TPU v7x, 32 devices: a whole 2x2x4 slice. The times are simulated.
32 devices in a mesh: row: 8 (over z, x), col: 4 (over y, core).
Axes of the slice: x: 2, y: 2, z: 4, core: 2. Of those that a mesh axis runs over, the one named last changes fastest.
Arguments:
- p_values: bfloat16 [96, 512, 128], P('row', 'col'), may hold values from -0.8984375 to 0.8984375
- p_where: int32 [96, 8], P('row', 'col'), may hold values from 0 to 63, as said below
- p_count: int32 [8, 4], P('row', 'col'), may hold values from 6 to 12, as said below
- h_values: bfloat16 [96, 512, 128], P('row', 'col'), may hold values from -3 to 3
- h_where: int32 [96, 8], P('row', 'col'), may hold values from 0 to 63, as said below
- h_count: int32 [8, 4], P('row', 'col'), may hold values from 6 to 12, as said below
Outputs:
- ph_values: bfloat16 [96, 512, 128], P('row', 'col')
- php_values: bfloat16 [96, 512, 128], P('row', 'col')
- energy: float32 [], replicated
Inputs may be any that keep to these rules, and one draw needn't show every extreme that they name: `p_where`: the 12 slots of the device of row index i and column index j name distinct blocks of its own tile: block rows i * 8 to i * 8 + 7 and the j-th of 4 equal ranges of block columns. `h_where`: as for p_where. `p_count`: some device has all 12 slots live. `h_count`: some device has all 12 slots live.
All inputs are finite; a program needn't handle non-finite values.
Results may differ from a plain program's by a relative error of at most 0.0049.
Values may be sent and summed in bfloat16 or wider, within the bound.
A program may use at most 64 MiB of HBM per device.

v0:
```python
import functools

import jax
import jax.numpy as jnp
from jax import lax
from jax.experimental import pallas as pl
from jax.experimental.pallas import tpu as pltpu
from jax.sharding import PartitionSpec as P

TILE = 8
CHUNKS = 6
IN_FLIGHT = 16
MESH = pl.DeviceIdType.MESH
ANY = pl.BlockSpec(memory_space=pl.ANY)
VMEM = pl.BlockSpec(memory_space=pltpu.VMEM)
SMEM = pl.BlockSpec(memory_space=pltpu.SMEM)


def at_row(r):
    return (r, lax.axis_index("col"))


def at_col(c):
    return (lax.axis_index("row"), c)


def remote(src, dst, send_sem, recv_sem, device):
    return pltpu.make_async_remote_copy(
        src_ref=src,
        dst_ref=dst,
        send_sem=send_sem,
        recv_sem=recv_sem,
        device_id=device,
        device_id_type=MESH,
    )


def greet(rows, cols):
    me_row, me_col = lax.axis_index("row"), lax.axis_index("col")
    barrier = pltpu.get_barrier_semaphore()
    for d in range(1, rows):
        pl.semaphore_signal(
            barrier, inc=1, device_id=at_row((me_row + d) % rows), device_id_type=MESH
        )
    for d in range(1, cols):
        pl.semaphore_signal(
            barrier, inc=1, device_id=at_col((me_col + d) % cols), device_id_type=MESH
        )
    pl.semaphore_wait(barrier, rows + cols - 2)


class ColumnGather:
    def __init__(self, rows, own, land, out, up_send, down_send, x_send, recv, local):
        self.own, self.land, self.out = own, land, out
        self.up_send, self.down_send, self.x_send = up_send, down_send, x_send
        self.recv, self.local = recv, local
        self.inner = 2 if rows % 2 == 0 else 1
        self.outer = rows // self.inner
        self.chunks = recv.shape[1]
        self.size = own.shape[0] // self.chunks
        self.me = lax.axis_index("row")
        self.x, self.z = self.me % self.inner, self.me // self.inner
        self.cross_first = 1 if self.inner == 2 and self.chunks > 1 else 0

    def later(self, ch):
        return (ch + self.cross_first) % self.chunks

    def row(self, z, line):
        return z * self.inner + (self.x if line == 0 else self.inner - 1 - self.x)

    def part(self, ch):
        return pl.ds(ch * self.size, self.size)

    def copy(self, r, ch, own, way):
        sems, target = {
            "up": (self.up_send, self.me + self.inner),
            "down": (self.down_send, self.me - self.inner),
            "x": (self.x_send, self.row(self.z, 1)),
        }[way]
        part = self.part(ch)
        src = self.own.at[part] if own else self.land.at[r, part]
        return remote(src, self.land.at[r, part], sems.at[r, ch], self.recv.at[r, ch], at_row(target))

    def keep(self, r, ch):
        part = self.part(ch)
        return pltpu.make_async_copy(self.land.at[r, part], self.out.at[r, part], self.local.at[r, ch])

    def along(self, r, ch, own, act):
        @pl.when(self.z < self.outer - 1)
        def _():
            act(self.copy(r, ch, own, "up"))

        @pl.when(self.z > 0)
        def _():
            act(self.copy(r, ch, own, "down"))

    def arrive(self, r, ch):
        self.copy(r, ch, False, "x").wait_recv()
        self.keep(r, ch).start()

    def start(self):
        for ch in range(self.chunks):
            if self.inner == 2:
                self.copy(self.me, ch, True, "x").start()
            self.along(self.me, self.later(ch), True, lambda copy: copy.start())
        if self.cross_first:
            r = self.row(self.z, 1)
            self.arrive(r, 0)
            self.along(r, 0, False, lambda copy: copy.start())

    def pieces(self):
        lines = [(self.later(ch), 0) for ch in range(self.chunks)]
        return lines + [(0, 1)] * self.cross_first

    def relayed(self, d, side, ch, line, act):
        z = self.z - d if side == 0 else self.z + d
        there = self.z >= d if side == 0 else self.z + d < self.outer
        r = self.row(z, line)

        @pl.when(there)
        def _():
            if act == "start":
                self.arrive(r, ch)
            on = self.z < self.outer - 1 if side == 0 else self.z > 0

            @pl.when(on)
            def _():
                copy = self.copy(r, ch, False, "up" if side == 0 else "down")
                copy.start() if act == "start" else copy.wait_send()

            if self.inner == 2 and ch >= self.cross_first:
                copy = self.copy(r, ch, False, "x")
                copy.start() if act == "start" else copy.wait_send()

    def relay(self, d):
        for ch, line in self.pieces():
            for side in range(2):
                self.relayed(d, side, ch, line, "start")

    def finish(self):
        if self.inner == 2:
            for ch in range(self.cross_first, self.chunks):
                self.arrive(self.row(self.z, 1), ch)
            for d in range(1, self.outer):
                for side in range(2):
                    z = self.z - d if side == 0 else self.z + d
                    there = self.z >= d if side == 0 else self.z + d < self.outer

                    @pl.when(there)
                    def _():
                        for ch in range(self.cross_first, self.chunks):
                            self.arrive(self.row(z, 1), ch)
        for ch in range(self.chunks):
            if self.inner == 2:
                self.copy(self.me, ch, True, "x").wait_send()
            self.along(self.me, ch, True, lambda copy: copy.wait_send())
        if self.cross_first:
            self.along(self.row(self.z, 1), 0, False, lambda copy: copy.wait_send())
        for d in range(1, self.outer):
            for ch, line in self.pieces():
                for side in range(2):
                    self.relayed(d, side, ch, line, "wait")
        for r in range(self.inner * self.outer):
            @pl.when(r != self.me)
            def _():
                for ch in range(self.chunks):
                    self.keep(r, ch).wait()


def col_copies(cols, own, out, send, recv):
    me = lax.axis_index("col")
    made = []
    for d in range(1, cols):
        made.append(
            remote(own, out.at[me], send.at[d], recv.at[d], at_col((me + d) % cols))
        )
    return made


def row_copies(rows, own, out, send, recv):
    me = lax.axis_index("row")
    made = []
    for d in range(1, rows):
        made.append(
            remote(own, out.at[me], send.at[d], recv.at[d], at_row((me + d) % rows))
        )
    return made


def first_gather(
    rows, cols, p_ref, h_ref, meta_ref, prow, hcol, prow_meta, col_meta,
    land, up_send, down_send, x_send, recv, out_sems,
    p_send, p_recv, mc_send, mc_recv, mr_send, mr_recv, local,
):
    me_row, me_col = lax.axis_index("row"), lax.axis_index("col")
    keep = [
        pltpu.make_async_copy(h_ref, hcol.at[me_row], local.at[0]),
        pltpu.make_async_copy(p_ref, prow.at[me_col], local.at[1]),
        pltpu.make_async_copy(meta_ref, prow_meta.at[me_col], local.at[2]),
        pltpu.make_async_copy(meta_ref, col_meta.at[me_row], local.at[3]),
    ]
    greet(rows, cols)
    gather = ColumnGather(
        rows, h_ref, land, hcol, up_send, down_send, x_send, recv, out_sems
    )
    across = (
        col_copies(cols, p_ref, prow, p_send, p_recv)
        + col_copies(cols, meta_ref, prow_meta, mc_send, mc_recv)
        + row_copies(rows, meta_ref, col_meta, mr_send, mr_recv)
    )
    for copy in across + keep:
        copy.start()
    gather.start()
    for d in range(1, gather.outer):
        gather.relay(d)
    gather.finish()
    for copy in across + keep:
        copy.wait()


def second_gather(
    rows, cols, p_ref, f_ref, e_ref, frow, pcol, e_out,
    e_cols, e_rows, e_sum,
    land, up_send, down_send, x_send, recv, out_sems,
    p_send, p_recv, ec_send, ec_recv, er_send, er_recv, local,
):
    me_row, me_col = lax.axis_index("row"), lax.axis_index("col")
    keep = [
        pltpu.make_async_copy(p_ref, pcol.at[me_row], local.at[0]),
        pltpu.make_async_copy(f_ref, frow.at[me_col], local.at[1]),
    ]
    greet(rows, cols)
    energies = col_copies(cols, e_ref, e_cols, ec_send, ec_recv)
    for copy in energies:
        copy.start()
    gather = ColumnGather(
        rows, p_ref, land, pcol, up_send, down_send, x_send, recv, out_sems
    )
    across = col_copies(cols, f_ref, frow, p_send, p_recv)
    for copy in across + keep:
        copy.start()
    gather.start()
    e_cols[me_col] = e_ref[...]
    for copy in energies:
        copy.wait()
    total = e_cols[0]
    for c in range(1, cols):
        total = total + e_cols[c]
    e_sum[...] = total
    e_rows[me_row] = total
    if gather.outer > 1:
        gather.relay(1)
    sums = row_copies(rows, e_sum, e_rows, er_send, er_recv)
    for copy in sums:
        copy.start()
    for d in range(2, gather.outer):
        gather.relay(d)
    for copy in sums:
        copy.wait()
    total = e_rows[0]
    for r in range(1, rows):
        total = total + e_rows[r]
    e_out[...] = total
    gather.finish()
    for copy in across + keep:
        copy.wait()


def block_products(
    rows, cols, right_lane, with_trace, lmeta, rmeta, left, right, *rest
):
    if with_trace:
        out, e_out = rest[:2]
    else:
        e_in, out, e_out = rest[:3]
    acc, lbuf, rbuf, head, nxt, inner, mask, table, ml, mr, ms, sems = rest[-12:]
    slots = out.shape[0]
    i, j = lax.axis_index("row"), lax.axis_index("col")
    nblk = rows * TILE
    tile_cols = nblk // cols
    words = -(-nblk // 32)
    count_lane = 4 * slots
    acc[...] = jnp.zeros_like(acc)

    for t in range(TILE + 1):
        head[t] = -1

    for t in range(tile_cols * words + 1):
        mask[t] = 0

    @pl.loop(0, cols)
    def _(c):
        live = lmeta[c, 0, count_lane]
        for s in range(slots):
            row = jnp.where(s < live, lmeta[c, 0, s] - i * TILE, TILE)
            idx = c * slots + s
            inner[idx] = lmeta[c, 0, slots + s]
            nxt[idx] = head[row]
            head[row] = idx

    @pl.loop(0, rows)
    def _(r):
        live = rmeta[r, 0, count_lane + (1 if right_lane else 0)]
        for s in range(slots):
            k = rmeta[r, 0, right_lane + s]
            col = rmeta[r, 0, right_lane + slots + s] - j * tile_cols
            word = jnp.where(s < live, col * words + (k >> 5), tile_cols * words)
            mask[word] = mask[word] | (jnp.int32(1) << (k & 31))
            table[jnp.where(s < live, k * tile_cols + col, nblk * tile_cols)] = r * slots + s

    def find_slot(s, n):
        row = lmeta[j, 0, s] - i * TILE
        col = lmeta[j, 0, slots + s] - j * tile_cols

        def more(state):
            return state[0] >= 0

        def step(state):
            at, n = state
            k = inner[at]
            ml[n] = at
            mr[n] = table[k * tile_cols + col]
            ms[n] = s
            return nxt[at], n + ((mask[col * words + (k >> 5)] >> (k & 31)) & 1)

        return lax.while_loop(more, step, (head[row], n))[1]

    own_count = lmeta[j, 0, count_lane]
    found = lax.fori_loop(0, own_count, find_slot, jnp.int32(0))

    def fetch(base, m):
        a, b = ml[base + m], mr[base + m]
        return (
            pltpu.make_async_copy(left.at[a], lbuf.at[m], sems.at[0, m]),
            pltpu.make_async_copy(right.at[b], rbuf.at[m], sems.at[1, m]),
        )

    @pl.loop(0, (found + IN_FLIGHT - 1) // IN_FLIGHT)
    def _(chunk):
        base = chunk * IN_FLIGHT
        size = jnp.minimum(found - base, IN_FLIGHT)

        @pl.loop(0, size)
        def _(m):
            for copy in fetch(base, m):
                copy.start()

        @pl.loop(0, size)
        def _(m):
            for copy in fetch(base, m):
                copy.wait()
            s = ms[base + m]
            acc[s] += jnp.dot(lbuf[m], rbuf[m], preferred_element_type=jnp.float32)

    out[...] = acc[...].astype(out.dtype)
    if with_trace:
        size = acc.shape[1]
        e_out[...] = jnp.zeros_like(e_out)
        diagonal = lax.broadcasted_iota(jnp.int32, (size, size), 0) == lax.broadcasted_iota(
            jnp.int32, (size, size), 1
        )

        @pl.loop(0, own_count)
        def _(s):
            @pl.when(lmeta[j, 0, s] == lmeta[j, 0, slots + s])
            def _():
                e_out[...] += jnp.sum(jnp.where(diagonal, acc[s], 0.0))
    else:
        e_out[0, 0] = e_in[0, 0]


def per_device(rows, cols, p_values, p_where, p_count, h_values, h_where, h_count):
    slots, size, _ = p_values.shape
    dtype = p_values.dtype
    nblk = rows * TILE
    tile_cols = nblk // cols
    words = -(-nblk // 32)
    meta = jnp.concatenate(
        [p_where[:, 0], p_where[:, 1], h_where[:, 0], h_where[:, 1], p_count[0], h_count[0]]
    )
    meta = jnp.broadcast_to(jnp.pad(meta, (0, 128 - meta.shape[0]))[None, :], (8, 128))
    dma = pltpu.SemaphoreType.DMA
    chunks = CHUNKS if slots % CHUNKS == 0 else 1
    chunk_sems = [pltpu.VMEM((rows, slots, size, size), dtype)] + [dma((rows, chunks))] * 5
    col_sems = [dma((cols,)), dma((cols,))]
    row_sems = [dma((rows,)), dma((rows,))]
    tile = (slots, size, size)
    prow, hcol, prow_meta, col_meta = pl.pallas_call(
        functools.partial(first_gather, rows, cols),
        out_shape=[
            jax.ShapeDtypeStruct((cols,) + tile, dtype),
            jax.ShapeDtypeStruct((rows,) + tile, dtype),
            jax.ShapeDtypeStruct((cols, 8, 128), jnp.int32),
            jax.ShapeDtypeStruct((rows, 8, 128), jnp.int32),
        ],
        in_specs=[VMEM] * 3,
        out_specs=[ANY] * 4,
        scratch_shapes=chunk_sems + col_sems + col_sems + row_sems + [dma((4,))],
        compiler_params=pltpu.CompilerParams(collective_id=0, has_side_effects=True),
        name="first_gather",
    )(p_values, h_values, meta)

    def products(right_lane, with_trace, lmeta, rmeta, left, right, *more):
        smem = lambda n: pltpu.SMEM((n,), jnp.int32)
        most = slots * nblk + 1
        return pl.pallas_call(
            functools.partial(block_products, rows, cols, right_lane, with_trace),
            out_shape=[
                jax.ShapeDtypeStruct(tile, dtype),
                jax.ShapeDtypeStruct((8, 128) if with_trace else (1, 1), jnp.float32),
            ],
            in_specs=[SMEM, SMEM, ANY, ANY] + [SMEM] * len(more),
            out_specs=[VMEM, VMEM if with_trace else SMEM],
            scratch_shapes=[
                pltpu.VMEM(tile, jnp.float32),
                pltpu.VMEM((IN_FLIGHT, size, size), dtype),
                pltpu.VMEM((IN_FLIGHT, size, size), dtype),
                smem(TILE + 1),
                smem(cols * slots),
                smem(cols * slots),
                smem(tile_cols * words + 1),
                smem(nblk * tile_cols + 1),
                smem(most),
                smem(most),
                smem(most),
                dma((2, IN_FLIGHT)),
            ],
            name="products",
        )(
            lmeta,
            rmeta,
            left.reshape((cols * slots, size, size)),
            right.reshape((rows * slots, size, size)),
            *more,
        )

    ph_values, part = products(2 * slots, True, prow_meta, col_meta, prow, hcol)
    frow, pcol, energy = pl.pallas_call(
        functools.partial(second_gather, rows, cols),
        out_shape=[
            jax.ShapeDtypeStruct((cols,) + tile, dtype),
            jax.ShapeDtypeStruct((rows,) + tile, dtype),
            jax.ShapeDtypeStruct((8, 128), jnp.float32),
        ],
        in_specs=[VMEM] * 3,
        out_specs=[ANY, ANY, VMEM],
        scratch_shapes=[
            pltpu.VMEM((cols, 8, 128), jnp.float32),
            pltpu.VMEM((rows, 8, 128), jnp.float32),
            pltpu.VMEM((8, 128), jnp.float32),
        ]
        + chunk_sems + col_sems + col_sems + row_sems + [dma((2,))],
        compiler_params=pltpu.CompilerParams(collective_id=1, has_side_effects=True),
        name="second_gather",
    )(p_values, ph_values, part)
    php_values, energy = products(0, False, prow_meta, col_meta, frow, pcol, energy)
    return (ph_values, php_values, energy[0, 0])


def solution(mesh):
    placed = (
        P("row", "col", None),
        P("row", "col"),
        P("row", "col"),
        P("row", "col", None),
        P("row", "col"),
        P("row", "col"),
    )
    return jax.shard_map(
        functools.partial(per_device, mesh.shape["row"], mesh.shape["col"]),
        mesh=mesh,
        in_specs=placed,
        out_specs=(P("row", "col", None), P("row", "col", None), P()),
        check_vma=False,
    )
```

profile of v0, /device:TPU:0, one launch (start us, length us, event | category | flops | bytes accessed | tf_op | source)
XLA Modules:
  0.0 96.3 jit_solution(5317505110913825386)
XLA Ops:
  1.9 0.8 slice_bitcast_fusion
  2.7 0.1 concatenate.3
  2.8 0.6 broadcast_in_dim.2.meta_ref
  3.4 42.3 %first_gather.1 = (bf16[4,12,128,128]{3,2,1,0:T(8,128)(2,1)}, bf16[8,12,128,128]{3,2,1,0:T(8,128)(2,1)}, s32[4,8,128]{2,1,0:T(8,128)}, s32[8,8,128]{2,1,0:T(8,128)}) custom-call(bf16[12,128,128]{2,1,0:T(8,128)(2,1)} %p_ref.3, bf16[12,128,128]{2,1,0:T(8,128)(2,1)} %h_ref.1, s32[8,128]{1,0:T(8,128)} %broadcast_in_dim.2.meta_ref), custom_call_target="tpu_custom_call" | custom-call | tf_op jit(solution)/shard_map/first_gather/pallas_call | solution.py:388
  45.7 5.7 %products.2 = (bf16[12,128,128]{2,1,0:T(8,128)(2,1)}, f32[8,128]{1,0:T(8,128)}) custom-call(s32[4,8,128]{2,1,0:T(8,128)} %get-tuple-element.14.lmeta, s32[8,8,128]{2,1,0:T(8,128)} %get-tuple-element.15.rmeta, bf16[48,128,128]{2,1,0:T(8,128)(2,1)} %bitcast.20, bf16[96,128,128]{2,1,0:T(8,128)(2,1)} %bitcast.17), custom_call_target="tpu_custom_call" | custom-call | tf_op jit(solution)/shard_map/products/pallas_call | solution.py:406
  51.3 39.4 %second_gather.1 = (bf16[4,12,128,128]{3,2,1,0:T(8,128)(2,1)}, bf16[8,12,128,128]{3,2,1,0:T(8,128)(2,1)}, f32[8,128]{1,0:T(8,128)}) custom-call(bf16[12,128,128]{2,1,0:T(8,128)(2,1)} %p_ref.3, bf16[12,128,128]{2,1,0:T(8,128)(2,1)} %get-tuple-element.11.f_ref, f32[8,128]{1,0:T(8,128)} %get-tuple-element.19.e_ref), custom_call_target="tpu_custom_call" | custom-call | tf_op jit(solution)/shard_map/second_gather/pallas_call | solution.py:438
  90.8 5.6 %products.3 = (bf16[12,128,128]{2,1,0:T(8,128)(2,1)}, f32[1,1]{1,0:T(1,128)}) custom-call(s32[4,8,128]{2,1,0:T(8,128)} %get-tuple-element.14.lmeta, s32[8,8,128]{2,1,0:T(8,128)} %get-tuple-element.15.rmeta, bf16[48,128,128]{2,1,0:T(8,128)(2,1)} %bitcast.19, bf16[96,128,128]{2,1,0:T(8,128)(2,1)} %bitcast.18, f32[8,128]{1,0:T(8,128)} %get-tuple-element.22.rest_0_), custom_call_target="tpu_custom_call" | custom-call | tf_op jit(solution)/shard_map/products/pallas_call | solution.py:406
  (1 shorter events, 0.0 us)
where the time goes:
time: 96.6 us; the launch traced here: 96.3 us
  Pallas kernels  92.9 us (96%)
  between operations  1.95 us (2%)
  local copies, waits for them, and re-layouts  1.45 us (2%)
    pallas_call x1, Pallas kernels, per_device(): pl.pallas_call(functools.partial(first_gather, rows, cols), out_shape=[ja...  42.3 us
    pallas_call x1, Pallas kernels, per_device(): pl.pallas_call(functools.partial(second_gather, rows, cols), out_shape=[j...  39.4 us
    pallas_call x2, Pallas kernels, products(): pl.pallas_call(functools.partial(block_products, rows, cols, right_lane,...  11.2 us

commit v1 on v0

--- a/solution.py
+++ b/solution.py
@@ -369,7 +369,7 @@
         e_out[0, 0] = e_in[0, 0]
 
 
-def per_device(rows, cols, p_values, p_where, p_count, h_values, h_where, h_count):
+def dense_path(rows, cols, p_values, p_where, p_count, h_values, h_where, h_count):
     slots, size, _ = p_values.shape
     dtype = p_values.dtype
     nblk = rows * TILE
@@ -457,6 +457,568 @@
     return (ph_values, php_values, energy[0, 0])
 
 
+CAP_H_Z, CAP_P_Z = 18, 12
+CAP_H, CAP_P = 13, 9
+CAP_F = 5
+CAP_1, CAP_2 = 15, 13
+LIST = 16
+F32, BF16, I32 = jnp.float32, jnp.bfloat16, jnp.int32
+
+
+def log2(n):
+    return n.bit_length() - 1
+
+
+def power(n):
+    return n > 0 and n & (n - 1) == 0
+
+
+class Shape:
+    def __init__(self, rows, cols, slots, size):
+        self.rows, self.cols, self.slots, self.size = rows, cols, slots, size
+        self.devices = rows * cols
+        self.nblk = rows * TILE
+        self.inner = 2 if rows % 2 == 0 else 1
+        self.outer = rows // self.inner
+        self.group = min(cols, 4)
+        self.team = self.inner * self.group
+        self.strip = size // self.team
+        self.width = self.nblk // cols
+        self.chips = cols // 2
+        self.partner = slots
+        self.others = 2 * slots
+        self.row_n = self.outer - 1
+        self.row_m = self.row_n + self.inner
+        self.row_f = self.row_m + 2
+        self.table = -(-(self.row_f + self.chips - 1) // 8) * 8
+
+    def fits(self):
+        return (
+            power(self.rows)
+            and power(self.cols)
+            and self.cols >= 2
+            and self.rows >= 2
+            and self.nblk <= 128
+            and self.width * TILE <= 128
+            and self.slots <= 15
+            and self.strip % 16 == 0
+            and self.group * LIST <= 64
+        )
+
+
+def mm(a, b):
+    return lax.dot_general(a.astype(BF16), b.astype(BF16), (((1,), (0,)), ((), ())), preferred_element_type=F32)
+
+
+def mt(a, b):
+    return lax.dot_general(a.astype(BF16), b.astype(BF16), (((1,), (1,)), ((), ())), preferred_element_type=F32)
+
+
+def tm(a, b):
+    return lax.dot_general(a.astype(BF16), b.astype(BF16), (((0,), (0,)), ((), ())), preferred_element_type=F32)
+
+
+def ones(cond):
+    return jnp.where(cond, 1.0, 0.0).astype(F32)
+
+
+def iota(shape, dim):
+    return lax.broadcasted_iota(I32, shape, dim)
+
+
+def make_lists(sh, x, z, j, pw, p_count, message, tabv):
+    n, width = sh.nblk, sh.width
+    i = z * sh.inner + x
+    lw, ll = log2(width), 3 + log2(sh.inner)
+    r, l = iota((n, n), 0), iota((n, n), 1)
+    g = j // sh.group
+    eight = jnp.ones((8, n), F32)
+
+    a0, d0 = iota((sh.cols * n, sh.devices), 0), iota((sh.cols * n, sh.devices), 1)
+    pick = ones(d0 == ((a0 & (n - 1)) >> 3) * sh.cols + (a0 >> log2(n)))
+    spread = mm(pick, message)
+    a1, l1 = iota((sh.cols * n, 128), 0), iota((sh.cols * n, 128), 1)
+    spread = jnp.where((l1 >> lw) == (a1 & 7), spread, 0.0)
+    l2, m2 = iota((128, n), 0), iota((128, n), 1)
+    spread = mm(spread, ones((l2 & (width - 1)) == (m2 & (width - 1))))
+    both = jnp.zeros((n, n), F32)
+    for c in range(sh.cols):
+        both = both + jnp.where((l >> lw) == c, spread[c * n : (c + 1) * n], 0.0)
+    hs = jnp.floor(both * (1.0 / 16.0))
+    ps = both - 16.0 * hs
+    pm, hm = ones(ps > 0.5), ones(hs > 0.5)
+    fm = pm * ones(mm(pm, hm) > 0.5)
+    slot = {"H": hs - 1.0, "P": ps - 1.0}
+    live = {"H": hm, "P": pm}
+    left = {"H": pm, "P": fm}
+    lane_tile = l >> lw
+    group_tri = ones((lane_tile // sh.group == (r >> lw) // sh.group) & (r < l))
+    group_full = ones(lane_tile // sh.group == (r >> lw) // sh.group)
+    seg_tri = ones((lane_tile == (r >> lw)) & (r < l))
+    seg_full = ones(lane_tile == (r >> lw))
+    low = ones(l < r)
+    up = ones(r < l)
+    low_layer = ones((l < r) & ((l >> ll) == (r >> ll)))
+    in_group = ones(lane_tile // sh.group == g)
+    over = jnp.zeros((1, n), F32)
+
+    def count_over(over, v, pos, cap):
+        return over + jnp.sum(v * ones(pos > cap - 0.5), axis=0, keepdims=True)
+
+    def extract(starts, counts, v, pos, payloads, size):
+        at = iota((size, n), 0).astype(F32)
+        rows = ones((starts <= at) & (at < starts + counts))
+        hit = mm(rows, v * (pos + 1.0)) == at + 1.0
+        return rows, [jnp.where(hit, mm(rows, p), 0.0) for p in payloads]
+
+    def put(row, lane, value, count):
+        tabv[row : row + 1, lane : lane + count] = value[0:1, 0:count].astype(I32)
+
+    team = ((r >> 3) & (sh.inner - 1)) * sh.group + lane_tile % sh.group
+    pos_mine = {}
+    for kind, cap_z, cap, shift in (("H", CAP_H_Z, CAP_H, 0), ("P", CAP_P_Z, CAP_P, 64)):
+        near = (team * sh.slots).astype(F32) + slot[kind]
+        need = []
+        for xd in range(sh.inner):
+            here = ones((r >> 3) == z * sh.inner + xd)
+            need.append(ones(tm(left[kind] * here, pm) > 0.5) * live[kind])
+        for dz in range(sh.outer):
+            if dz == 0:
+                v = need[0] if sh.inner == 1 else jnp.maximum(need[0], need[1])
+            else:
+                there = ones((r >> ll) == (z + dz) % sh.outer)
+                v = ones(tm(left[kind] * there, pm) > 0.5) * live[kind] * ones((r >> ll) == z)
+            v = v * in_group
+            pos = mm(v, group_tri) + mm(low_layer, mm(v, group_full))
+            if dz == 0:
+                pos_z = pos
+                continue
+            counts = mt(eight, v)
+            starts = mm(counts, up)
+            size = -(-cap_z // 8) * 8
+            _, (found,) = extract(starts[0:1], counts[0:1], v, pos, [near], size)
+            put(dz - 1, shift, mt(eight, found), size)
+            over = count_over(over, v, pos, cap_z)
+        far = (sh.team * sh.slots + (r >> ll) * cap_z).astype(F32) + jnp.minimum(pos_z, cap_z - 1.0)
+        payload = jnp.where((r >> ll) == z, near, far)
+        mine = jnp.zeros((n, n), F32)
+        e0, e1 = iota((8, n), 0), iota((8, n), 1)
+        columns = ones(((e1 >> lw) == g * sh.group + e0) & (e0 < sh.group))
+        for xd in range(sh.inner):
+            v = need[xd]
+            pos = mm(v, seg_tri) + mm(low, mm(v, seg_full))
+            over = count_over(over, v, pos, cap)
+            mine = mine + jnp.where(x == xd, 1.0, 0.0) * pos
+            counts = mt(columns, v)
+            starts = mm(counts, up)
+            rows = []
+            at = iota((LIST, n), 0).astype(F32)
+            for a in range(sh.group):
+                rows.append(ones((starts[a : a + 1] <= at) & (at < starts[a : a + 1] + counts[a : a + 1])))
+            rows = jnp.concatenate(rows, axis=0)
+            total = sh.group * LIST
+            t0, t1 = iota((total, n), 0), iota((total, n), 1)
+            here = (mm(rows, v * (pos + 1.0)) == ((t0 & (LIST - 1)) + 1).astype(F32)) & (
+                (t1 >> lw) == g * sh.group + (t0 >> log2(LIST))
+            )
+            found = mt(eight, jnp.where(here, mm(rows, payload), 0.0))
+            put(sh.row_n + xd, shift, found, total)
+        pos_mine[kind] = jnp.minimum(mine, cap - 1.0)
+
+    chip = j // 2
+    lane_chip = lane_tile // 2
+    in_rows = ones((r >> 3) == i)
+    for dc in range(sh.chips):
+        there = ones(lane_chip == (chip + dc) % sh.chips)
+        v = ones(mt(pm * there, pm) > 0.5) * fm * in_rows
+        pos = mm(v, seg_tri) + mm(low, mm(v, seg_full))
+        if dc == 0:
+            pos_f = jnp.minimum(pos, CAP_F - 1.0)
+            continue
+        v = v * ones(lane_tile == j)
+        counts = mt(eight, v)
+        starts = mm(counts, up)
+        _, (found,) = extract(starts[0:1], counts[0:1], v, pos, [slot["P"]], 8)
+        put(sh.row_f + dc - 1, 0, mt(eight, found), 8)
+        over = count_over(over, v, pos, CAP_F)
+
+    s0, s1 = iota((LIST, n), 0), iota((LIST, n), 1)
+    row_of = jnp.full((LIST, n), -1, I32)
+    col_of = jnp.full((LIST, n), -1, I32)
+    for s in range(sh.slots):
+        row_of = jnp.where((s0 == s) & (s < p_count[0, 0]), pw[s, 0], row_of)
+        col_of = jnp.where((s0 == s) & (s < p_count[0, 0]), pw[s, 1], col_of)
+    oh_row, oh_col = ones(row_of == s1), ones(col_of == s1)
+    k_tile = lane_tile.astype(F32)
+    left_1 = k_tile * sh.slots + slot["P"]
+    left_2 = jnp.where(
+        lane_tile == j,
+        slot["P"],
+        jnp.where(lane_chip == chip, sh.partner + slot["P"], sh.others + k_tile * CAP_F + pos_f),
+    )
+    q0, q1 = iota((LIST, LIST), 0), iota((LIST, LIST), 1)
+    for step, (kind, from_left, cap) in enumerate((("H", left_1, CAP_1), ("P", left_2, CAP_2))):
+        w = mm(oh_row, left[kind]) * mt(oh_col, live[kind])
+        li = mm(oh_row, from_left * pm)
+        ri = mt(oh_col, pos_mine[kind])
+        counts_s = mm(w, jnp.ones((n, n), F32))
+        pos = mm(w, up) + mm(ones(q1 < q0), counts_s)
+        over = count_over(over, w, pos, cap)
+        counts = mt(eight, w)
+        starts = mm(counts, ones(q0 < q1))
+        at = q0.astype(F32)
+        rows = ones((starts[0:1] <= at) & (at < starts[0:1] + counts[0:1]))
+        hit = mm(rows, w * (pos + 1.0)) == s0.astype(F32) + 1.0
+        row = sh.row_m + step
+        put(row, 0, mt(eight, jnp.where(hit, mm(rows, li), 0.0)), LIST)
+        put(row, 16, mt(eight, jnp.where(hit, mm(rows, ri), 0.0)), LIST)
+        keep = rows * ones(at > starts[0:1])
+        put(row, 32, mt(jnp.ones((8, LIST), F32), keep), LIST)
+        last = jnp.where(counts > 0.5, jnp.minimum(starts + counts - 1.0, cap), 1.0 * cap)
+        put(row, 48, last, LIST)
+    return over
+
+
+def sparse_products(
+    sh, p_ref, h_ref, pw, pc, hw, hc, ph_out, php_out, e_out,
+    message, messages, near_h, near_p, store_h, store_p, prow, pack_hz, pack_pz, pack_h, pack_p,
+    land_h, land_p, terms_1, terms_2, fstore, pack_f, tabv, tab, emsg, emsgs, esum,
+    m_send, m_recv, s_send, s_recv, p_send, p_fwd, p_recv, z_send, z_recv,
+    t_send, t_recv, f_send, f_fwd, f_recv, e_send, e_recv, t_copy,
+):
+    i, j = lax.axis_index("row"), lax.axis_index("col")
+    x, z = i % sh.inner, i // sh.inner
+    me = i * sh.cols + j
+    g, a = j // sh.group, j % sh.group
+    chip, core = j // 2, j % 2
+    mate = (i, chip * 2 + 1 - core)
+    team = x * sh.group + a
+    slots, strip, size = sh.slots, sh.strip, sh.size
+    all_but_me = sh.devices - 1
+
+    def device(d):
+        t = (me + d) % sh.devices
+        return (t // sh.cols, t % sh.cols)
+
+    def member(d):
+        q = (team + d) % sh.team
+        return q, (z * sh.inner + q // sh.group, g * sh.group + q % sh.group)
+
+    def in_strip(q):
+        return pl.ds(pl.multiple_of(q * strip, strip), strip)
+
+    lane = iota((1, 128), 1)
+    packed = jnp.zeros((1, 128), F32)
+    for where, count, scale in ((pw, pc, 1.0), (hw, hc, 16.0)):
+        for s in range(slots):
+            at = (where[s, 0] - i * TILE) * sh.width + where[s, 1] - j * sh.width
+            packed = packed + jnp.where((lane == at) & (s < count[0, 0]), scale * (s + 1), 0.0)
+    message[0] = packed
+    messages[me] = packed
+
+    barrier = pltpu.get_barrier_semaphore()
+
+    @pl.loop(1, sh.devices)
+    def _(d):
+        pl.semaphore_signal(barrier, inc=1, device_id=device(d), device_id_type=MESH)
+
+    for s in range(slots):
+        near_h[team * slots + s] = h_ref[s, in_strip(team), :]
+        near_p[team * slots + s] = p_ref[s, in_strip(team), :]
+        prow[j * slots + s] = p_ref[s]
+    pl.semaphore_wait(barrier, all_but_me)
+
+    def tell(d):
+        return remote(message.at[pl.ds(0, 1)], messages.at[pl.ds(me, 1)], m_send, m_recv, device(d))
+
+    @pl.loop(1, sh.devices)
+    def _(d):
+        tell(d).start()
+
+    def strips(d, which):
+        q, dev = member(d)
+        ref, near = ((h_ref, near_h), (p_ref, near_p))[which]
+        return remote(
+            ref.at[:, in_strip(q), :], near.at[pl.ds(team * slots, slots)],
+            s_send.at[which, d], s_recv.at[which, team], dev,
+        )
+
+    def strips_in(d, which):
+        q, dev = member(d)
+        ref, near = ((h_ref, near_h), (p_ref, near_p))[which]
+        return remote(
+            ref.at[:, in_strip(q), :], near.at[pl.ds(q * slots, slots)],
+            s_send.at[which, d], s_recv.at[which, q], dev,
+        )
+
+    for which in range(2):
+        for d in range(1, sh.team):
+            strips(d, which).start()
+
+    def other(dc):
+        c = (chip + dc) % sh.chips
+        return c, c * 2 + core
+
+    def p_block(col):
+        return prow.at[pl.ds(col * slots, slots)]
+
+    def p_out(dc):
+        return remote(p_ref, p_block(j), p_send.at[dc], p_recv.at[j], (i, other(dc)[1]) if dc else mate)
+
+    def p_in(col):
+        return remote(p_ref, p_block(col), p_send.at[0], p_recv.at[col], mate)
+
+    def p_forward(dc):
+        col = other(dc)[1]
+        return remote(p_block(col), p_block(col), p_fwd.at[dc], p_recv.at[col], mate)
+
+    for dc in range(sh.chips):
+        p_out(dc).start()
+
+    def bulk(ref, sem):
+        part = ref.at[pl.ds(0, all_but_me)]
+        return pltpu.make_async_copy(part, part, sem)
+
+    bulk(messages, m_recv).wait()
+    over = make_lists(sh, x, z, j, pw, pc, messages[:, 0, :], tabv)
+    table = pltpu.make_async_copy(tabv, tab, t_copy)
+    table.start()
+    table.wait()
+
+    def entry(ref, row, lane):
+        return ref[jnp.minimum(jnp.maximum(tab[row, lane], 0), ref.shape[0] - 1)]
+
+    kinds = (
+        (store_h, pack_hz, pack_h, land_h, CAP_H_Z, CAP_H, near_h),
+        (store_p, pack_pz, pack_p, land_p, CAP_P_Z, CAP_P, near_p),
+    )
+
+    def zone(which, layer):
+        store, cap = kinds[which][0], kinds[which][4]
+        return store.at[pl.ds(sh.team * slots + layer * cap, cap)]
+
+    def across(which, dz):
+        pack = kinds[which][1]
+        zd = (z + dz) % sh.outer
+        return remote(
+            pack.at[dz - 1], zone(which, z), z_send.at[which, dz], z_recv.at[which, z],
+            (zd * sh.inner + x, j),
+        )
+
+    def across_in(which, dz):
+        pack = kinds[which][1]
+        zs = (z + dz) % sh.outer
+        return remote(
+            pack.at[dz - 1], zone(which, zs), z_send.at[which, dz], z_recv.at[which, zs],
+            (zs * sh.inner + x, j),
+        )
+
+    for which in range(2):
+        store, pack, _, _, cap, _, near = kinds[which]
+        for d in range(1, sh.team):
+            strips_in(d, which).wait_recv()
+        for dz in range(1, sh.outer):
+            for k in range(cap):
+                pack[dz - 1, k] = entry(near, dz - 1, 64 * which + k)
+        for dz in range(1, sh.outer):
+            across(which, dz).start()
+        store[0 : sh.team * slots] = near[...]
+
+    for dc in range(1, sh.chips):
+        p_in(other(dc)[1]).wait_recv()
+        p_forward(dc).start()
+
+    def part(which, d):
+        pack, land = kinds[which][2], kinds[which][3]
+        _, dev = member(d)
+        return remote(
+            pack.at[d - 1], land.at[:, in_strip(team), :], t_send.at[which, d], t_recv.at[which, team], dev
+        )
+
+    def part_in(which, d):
+        pack, land = kinds[which][2], kinds[which][3]
+        q, dev = member(d)
+        return remote(
+            pack.at[d - 1], land.at[:, in_strip(q), :], t_send.at[which, d], t_recv.at[which, q], dev
+        )
+
+    for which in range(2):
+        store, _, pack, land, _, cap, _ = kinds[which]
+        for dz in range(1, sh.outer):
+            across_in(which, dz).wait_recv()
+
+        @pl.loop(1, sh.team)
+        def _(d):
+            q, _ = member(d)
+            for k in range(cap):
+                lane = 64 * which + (q % sh.group) * LIST + k
+                pack[d - 1, k] = entry(store, sh.row_n + q // sh.group, lane)
+
+        for d in range(1, sh.team):
+            part(which, d).start()
+        for k in range(cap):
+            land[k, in_strip(team), :] = entry(store, sh.row_n + x, 64 * which + a * LIST + k)
+
+    def multiply(step, left, right, terms, cap):
+        row = sh.row_m + step
+        acc = None
+        for k in range(cap):
+            d = jnp.dot(entry(left, row, k), entry(right, row, 16 + k), preferred_element_type=F32)
+            acc = d if acc is None else d + acc * tab[row, 32 + k].astype(F32)
+            terms[k] = acc
+        terms[cap] = jnp.zeros((size, size), F32)
+
+    p_in(mate[1]).wait_recv()
+    for dc in range(1, sh.chips):
+        p_in(other(dc)[0] * 2 + 1 - core).wait_recv()
+    for d in range(1, sh.team):
+        part_in(0, d).wait_recv()
+    multiply(0, prow, land_h, terms_1, CAP_1)
+    trace = jnp.zeros((size, size), F32)
+    for s in range(slots):
+        value = entry(terms_1, sh.row_m, 48 + s)
+        trace = trace + value * jnp.where(pw[s, 0] == pw[s, 1], 1.0, 0.0)
+        rounded = value.astype(BF16)
+        fstore[s] = rounded
+        ph_out[s] = rounded
+
+    def f_block(col):
+        return fstore.at[pl.ds(sh.others + col * CAP_F, CAP_F)]
+
+    def f_out(dc):
+        return remote(pack_f.at[dc - 1], f_block(j), f_send.at[dc], f_recv.at[j], (i, other(dc)[1]))
+
+    def f_in(dc):
+        return remote(pack_f.at[dc - 1], f_block(other(dc)[1]), f_send.at[dc], f_recv.at[other(dc)[1]], (i, other(dc)[1]))
+
+    def f_forward(dc):
+        col = other(dc)[1]
+        return remote(f_block(col), f_block(col), f_fwd.at[dc], f_recv.at[col], mate)
+
+    def f_forward_in(dc):
+        col = other(dc)[0] * 2 + 1 - core
+        return remote(f_block(col), f_block(col), f_fwd.at[dc], f_recv.at[col], mate)
+
+    own_f = remote(
+        ph_out, fstore.at[pl.ds(sh.partner, slots)], f_send.at[0], f_recv.at[sh.cols], mate
+    )
+    for dc in range(1, sh.chips):
+        for k in range(CAP_F):
+            pack_f[dc - 1, k] = entry(ph_out, sh.row_f + dc - 1, k)
+    for dc in range(1, sh.chips):
+        f_out(dc).start()
+    own_f.start()
+
+    diagonal = iota((size, size), 0) == iota((size, size), 1)
+    emsg[0, 0] = jnp.sum(jnp.where(diagonal, trace, 0.0), axis=0, keepdims=True)
+    emsg[0, 1] = jnp.sum(over, axis=1, keepdims=True) + jnp.zeros((1, 128), F32)
+    emsgs[me] = emsg[0]
+
+    def tell_energy(d):
+        return remote(emsg.at[pl.ds(0, 1)], emsgs.at[pl.ds(me, 1)], e_send, e_recv, device(d))
+
+    @pl.loop(1, sh.devices)
+    def _(d):
+        tell_energy(d).start()
+
+    for dc in range(1, sh.chips):
+        f_in(dc).wait_recv()
+        f_forward(dc).start()
+    for d in range(1, sh.team):
+        part_in(1, d).wait_recv()
+    own_f.wait_recv()
+    for dc in range(1, sh.chips):
+        f_forward_in(dc).wait_recv()
+    multiply(1, fstore, land_p, terms_2, CAP_2)
+    for s in range(slots):
+        php_out[s] = entry(terms_2, sh.row_m + 1, 48 + s).astype(BF16)
+
+    bulk(emsgs, e_recv).wait()
+    for line in range(2):
+        total = jnp.sum(emsgs[:, line], axis=0)
+        e_out[line : line + 1, :] = jnp.sum(total, axis=1, keepdims=True) + jnp.zeros((1, 128), F32)
+
+    bulk(messages, m_send).wait()
+    bulk(emsgs, e_send).wait()
+    for which in range(2):
+        for d in range(1, sh.team):
+            strips(d, which).wait_send()
+            part(which, d).wait_send()
+        for dz in range(1, sh.outer):
+            across(which, dz).wait_send()
+    for dc in range(sh.chips):
+        p_out(dc).wait_send()
+    own_f.wait_send()
+    for dc in range(1, sh.chips):
+        p_forward(dc).wait_send()
+        f_out(dc).wait_send()
+        f_forward(dc).wait_send()
+
+
+def sparse_path(sh, p_values, p_where, p_count, h_values, h_where, h_count):
+    slots, size, strip = sh.slots, sh.size, sh.strip
+    block, piece = (size, size), (strip, size)
+    bf = lambda *shape: pltpu.VMEM(shape, BF16)
+    f32 = lambda *shape: pltpu.VMEM(shape, F32)
+    dma = pltpu.SemaphoreType.DMA
+    near = sh.team * slots
+    away = max(sh.outer - 1, 1)
+    chips = max(sh.chips - 1, 1)
+    tile = jax.ShapeDtypeStruct((slots,) + block, BF16)
+    return pl.pallas_call(
+        functools.partial(sparse_products, sh),
+        out_shape=[tile, tile, jax.ShapeDtypeStruct((2, 128), F32)],
+        in_specs=[VMEM, VMEM, SMEM, SMEM, SMEM, SMEM],
+        out_specs=[VMEM, VMEM, VMEM],
+        scratch_shapes=[
+            f32(1, 1, 128),
+            f32(sh.devices, 1, 128),
+            bf(near, *piece),
+            bf(near, *piece),
+            bf(near + sh.outer * CAP_H_Z, *piece),
+            bf(near + sh.outer * CAP_P_Z, *piece),
+            bf(sh.cols * slots, *block),
+            bf(away, CAP_H_Z, *piece),
+            bf(away, CAP_P_Z, *piece),
+            bf(sh.team, CAP_H, *piece),
+            bf(sh.team, CAP_P, *piece),
+            bf(CAP_H, *block),
+            bf(CAP_P, *block),
+            f32(CAP_1 + 1, *block),
+            f32(CAP_2 + 1, *block),
+            bf(sh.others + sh.cols * CAP_F, *block),
+            bf(chips, CAP_F, *block),
+            pltpu.VMEM((sh.table, 128), I32),
+            pltpu.SMEM((sh.table, 128), I32),
+            f32(1, 2, 1, 128),
+            f32(sh.devices, 2, 1, 128),
+            f32(8, 128),
+            dma, dma,
+            dma((2, sh.team)), dma((2, sh.team)),
+            dma((sh.chips,)), dma((sh.chips,)), dma((sh.cols,)),
+            dma((2, sh.outer)), dma((2, sh.outer)),
+            dma((2, sh.team)), dma((2, sh.team)),
+            dma((sh.chips,)), dma((sh.chips,)), dma((sh.cols + 1,)),
+            dma, dma, dma,
+        ],
+        compiler_params=pltpu.CompilerParams(collective_id=2, has_side_effects=True),
+        name="sparse_products",
+    )(p_values, h_values, p_where, p_count, h_where, h_count)
+
+
+def per_device(rows, cols, *args):
+    slots, size, _ = args[0].shape
+    sh = Shape(rows, cols, slots, size)
+    if not sh.fits():
+        return dense_path(rows, cols, *args)
+    ph, php, summary = sparse_path(sh, *args)
+    return lax.cond(
+        summary[1, 0] > 0.0,
+        lambda: dense_path(rows, cols, *args),
+        lambda: (ph, php, summary[0, 0]),
+    )
+
+
 def solution(mesh):
     placed = (
         P("row", "col", None),

time: 96.6 us -> 54 us (0.56)
  Pallas kernels: 92.9 us -> 44.1 us
  local copies, waits for them, and re-layouts: 1.45 us -> 6.26 us
    pallas_call x4 -> x1, Pallas kernels: 92.9 us -> 44.1 us  [sparse_path(): pl.pallas_call(functools.partial(sparse_products, sh), out_shape=[tile, t...]
    unnamed x0 -> x4, local copies, waits for them, and re-layouts: none -> 5.23 us
    slice x0 -> x2, local copies, waits for them, and re-layouts: none -> 1.03 us  [the longest x1 0.51 us: per_device(): summary[1, 0] > 0.0]
where the time goes in v1:
time: 54 us; the launch traced here: 53 us
  Pallas kernels  44.1 us (82%)
  local copies, waits for them, and re-layouts  6.26 us (12%)
  between operations  2.59 us (5%)
    pallas_call x1, Pallas kernels, sparse_path(): pl.pallas_call(functools.partial(sparse_products, sh), out_shape=[tile, t...  44.1 us
    unnamed x4, local copies, waits for them, and re-layouts  5.23 us

profile of v1, /device:TPU:0, one launch (start us, length us, event | category | flops | bytes accessed | tf_op | source)
XLA Modules:
  0.0 53.0 jit_solution(7016827147439861702)
XLA Ops:
  1.9 1.4 %copy.11.pw = s32[12,2]{1,0:T(8,128)} copy(s32[12,2]{0,1:T(2,128)} %param.9) | data formatting | bytes 192 | tf_op args[1]
  3.3 1.4 %copy.12.hw = s32[12,2]{1,0:T(8,128)} copy(s32[12,2]{0,1:T(2,128)} %param.12) | data formatting | bytes 192 | tf_op args[4]
  4.6 44.1 %sparse_products.1 = (bf16[12,128,128]{2,1,0:T(8,128)(2,1)}, bf16[12,128,128]{2,1,0:T(8,128)(2,1)S(1)}, f32[2,128]{1,0:T(2,128)S(1)}) custom-call(bf16[12,128,128]{2,1,0:T(8,128)(2,1)} %p_ref.1, bf16[12,128,128]{2,1,0:T(8,128)(2,1)} %h_ref.1, s32[12,2]{1,0:T(8,128)} %copy.11.pw, s32[1,1]{1,0:T(1,128)S(6)} %copy.21.pc, s32[12,2]{1,0:T(8,128)} %copy.12.hw, ...), custom_call_target="tpu_custom_call" | custom-call | tf_op jit(solution)/shard_map/sparse_products/pallas_call | solution.py:968
  48.8 0.5 slice.18
  50.0 0.5 conditional.1
  50.0 0.5 slice.12
  50.5 1.8 %copy.23 = bf16[12,128,128]{2,1,0:T(8,128)(2,1)} copy(bf16[12,128,128]{2,1,0:T(8,128)(2,1)} %get-tuple-element.63) | data formatting | bytes 786432
  52.2 0.7 %copy.24 = bf16[12,128,128]{2,1,0:T(8,128)(2,1)} copy(bf16[12,128,128]{2,1,0:T(8,128)(2,1)S(1)} %get-tuple-element.64) | data formatting | bytes 786432

commit v2 on v0

--- a/solution.py
+++ b/solution.py
@@ -369,7 +369,7 @@
         e_out[0, 0] = e_in[0, 0]
 
 
-def per_device(rows, cols, p_values, p_where, p_count, h_values, h_where, h_count):
+def dense_path(rows, cols, p_values, p_where, p_count, h_values, h_where, h_count):
     slots, size, _ = p_values.shape
     dtype = p_values.dtype
     nblk = rows * TILE
@@ -457,6 +457,634 @@
     return (ph_values, php_values, energy[0, 0])
 
 
+CAP_H_Z, CAP_P_Z = 17, 12
+CAP_H, CAP_P = 14, 9
+CAP_R, CAP_V = 7, 7
+CAP_1, CAP_2 = 18, 12
+LIST, LIST_Z, LIST_1, EIGHT = 16, 24, 24, 8
+F32, BF16, I32 = jnp.float32, jnp.bfloat16, jnp.int32
+
+
+def log2(n):
+    return n.bit_length() - 1
+
+
+def power(n):
+    return n > 0 and n & (n - 1) == 0
+
+
+class Shape:
+    def __init__(self, rows, cols, slots, size):
+        self.rows, self.cols, self.slots, self.size = rows, cols, slots, size
+        self.devices = rows * cols
+        self.nblk = rows * TILE
+        self.inner = 2 if rows % 2 == 0 else 1
+        self.outer = rows // self.inner
+        self.layer = self.inner * TILE
+        self.team = self.inner * cols
+        self.strip = size // self.team
+        self.width = self.nblk // cols
+        self.chips = cols // 2
+        self.others = 2 * slots
+
+    def fits(self):
+        return (
+            power(self.rows)
+            and power(self.cols)
+            and self.cols >= 2
+            and self.outer >= 2
+            and self.nblk <= 64
+            and self.width * TILE <= 128
+            and self.slots <= 15
+            and self.strip % 16 == 0
+            and self.team * LIST <= 128
+            and (self.outer - 1) * LIST_Z <= 128
+            and (self.chips - 1) * EIGHT <= 128
+        )
+
+
+def mm(a, b):
+    return lax.dot_general(a.astype(BF16), b.astype(BF16), (((1,), (0,)), ((), ())), preferred_element_type=F32)
+
+
+def mt(a, b):
+    return lax.dot_general(a.astype(BF16), b.astype(BF16), (((1,), (1,)), ((), ())), preferred_element_type=F32)
+
+
+def tm(a, b):
+    return lax.dot_general(a.astype(BF16), b.astype(BF16), (((0,), (0,)), ((), ())), preferred_element_type=F32)
+
+
+def ones(cond):
+    return jnp.where(cond, 1.0, 0.0).astype(F32)
+
+
+def iota(shape, dim):
+    return lax.broadcasted_iota(I32, shape, dim)
+
+
+def block_index(shape, dim, size):
+    return iota(shape, dim) // size
+
+
+def total_over(counts, starts, cap):
+    over = ones(starts + counts > cap + 0.5)
+    return jnp.sum(jnp.sum(over, axis=0, keepdims=True), axis=1, keepdims=True)
+
+
+def stack(parts):
+    return jnp.concatenate(parts, axis=0)
+
+
+class Lists:
+    def __init__(self, sh, x, z, j, message):
+        self.sh, self.x, self.z, self.j = sh, x, z, j
+        n, width, layer = sh.nblk, sh.width, sh.layer
+        lw = log2(width)
+        r, l = iota((n, n), 0), iota((n, n), 1)
+        a0, d0 = iota((sh.cols * n, sh.devices), 0), iota((sh.cols * n, sh.devices), 1)
+        spread = mm(ones(d0 == ((a0 & (n - 1)) >> 3) * sh.cols + (a0 >> log2(n))), message)
+        a1, l1 = iota((sh.cols * n, 128), 0), iota((sh.cols * n, 128), 1)
+        spread = jnp.where((l1 >> lw) == (a1 & 7), spread, 0.0)
+        l2, m2 = iota((128, n), 0), iota((128, n), 1)
+        spread = mm(spread, ones((l2 & (width - 1)) == (m2 & (width - 1))))
+        both = jnp.zeros((n, n), F32)
+        for c in range(sh.cols):
+            both = both + jnp.where((l >> lw) == c, spread[c * n : (c + 1) * n], 0.0)
+        hs = jnp.floor(both * (1.0 / 16.0))
+        ps = both - 16.0 * hs
+        self.pm, self.hm = ones(ps > 0.5), ones(hs > 0.5)
+        self.fm = self.pm * ones(mm(self.pm, self.hm) > 0.5)
+        self.up, self.low = ones(r < l), ones(l < r)
+        self.low_layer = ones((l < r) & (l // layer == r // layer))
+        self.full = jnp.ones((n, n), F32)
+        self.r, self.l, self.lane_tile = r, l, l >> lw
+        team = ((r >> 3) & (sh.inner - 1)) * sh.cols + self.lane_tile
+        at = (team * sh.slots).astype(F32)
+        self.near = {"H": at + hs - 1.0, "P": at + ps - 1.0}
+        s0, s1 = iota((layer, n), 0), iota((layer, n), 1)
+        self.sel = ones(s1 == z * layer + s0)
+        self.row_i, self.row_tile = s0, (s1 >> lw)
+        self.p_layer, self.f_layer = mm(self.sel, self.pm), mm(self.sel, self.fm)
+        self.slot_layer = mm(self.sel, ps) - 1.0
+
+    def enumerate(self, v, count, lane_pos=None):
+        k, n = v.shape
+        counts = mt(jnp.ones((count, n), F32), v)
+        a, b = iota((k, k), 0), iota((k, k), 1)
+        starts = mm(counts, ones(a < b))
+        at = iota((count, k), 0).astype(F32)
+        rows = ones((starts <= at) & (at < starts + counts))
+        local = mm(rows * (at - starts + 1.0), jnp.ones((k, n), F32))
+        if lane_pos is None:
+            lane_pos = mm(v, self.up)
+        found = mm(rows, v * (lane_pos + 1.0))
+        lanes = ones((found == local) & (local > 0.5))
+        return rows, lanes, counts, starts, lane_pos
+
+    def position(self, v, low):
+        return mm(v, self.up) + mm(low, mm(v, self.full))
+
+    def across(self, tab):
+        sh, z, layer, n = self.sh, self.z, self.sh.layer, self.sh.nblk
+        p_s, f_s = mt(self.sel, self.pm), mt(self.sel, self.fm)
+        i_layer = self.l[0:layer] // layer
+        lhs, live, pay = [], [], []
+        for kind, left, right in (("H", p_s, self.hm), ("P", f_s, self.pm)):
+            live_kind, pay_kind = mm(self.sel, right), mm(self.sel, self.near[kind])
+            for dz in range(1, sh.outer):
+                lhs.append(left * ones(i_layer == (z + dz) % sh.outer))
+                live.append(live_kind)
+                pay.append(pay_kind)
+        v = ones(mm(stack(lhs), self.pm) > 0.5) * stack(live)
+        k = v.shape[0]
+        lists = 2 * (sh.outer - 1)
+        a, b = iota((k, k), 0), iota((k, k), 1)
+        counts = mt(jnp.ones((EIGHT, n), F32), v)
+        starts = mm(counts, ones((a < b) & (a // layer == b // layer)))
+        t0 = iota((lists * LIST_Z, k), 0)
+        at = (t0 % LIST_Z).astype(F32)
+        rows = ones(
+            (starts[0:1] <= at)
+            & (at < starts[0:1] + counts[0:1])
+            & (t0 // LIST_Z == block_index((lists * LIST_Z, k), 1, layer))
+        )
+        local = mm(rows * (at - starts[0:1] + 1.0), jnp.ones((k, n), F32))
+        found = mm(rows, v * (mm(v, self.up) + 1.0))
+        picked = jnp.where((found == local) & (local > 0.5), mm(rows, stack(pay)), 0.0)
+        half = (sh.outer - 1) * LIST_Z
+        for which in range(2):
+            line = mt(jnp.ones((EIGHT, n), F32), picked[which * half : (which + 1) * half])
+            tab[which : which + 1, 0:half] = line[0:1].astype(I32)
+        lane_h = block_index((EIGHT, k), 1, layer) < sh.outer - 1
+        cap = jnp.where(lane_h, 1.0 * CAP_H_Z, 1.0 * CAP_P_Z)
+        return total_over(counts - cap, starts, 0.0)
+
+    def row_lists(self, tab):
+        sh, x, j, layer, n = self.sh, self.x, self.j, self.sh.layer, self.sh.nblk
+        tiles = [ones(self.row_tile == c) for c in range(sh.cols)]
+        wide = stack([self.p_layer * t for t in tiles])
+        passed = ones(mt(wide, self.pm) > 0.5) * stack([self.f_layer] * sh.cols)
+        own = wide
+        self.outputs = jnp.maximum(own, passed)
+        self.remote_f = passed * (1.0 - ones(stack([t for t in tiles]) > 0.5))
+        reads = ones(mt(self.outputs, self.hm) > 0.5) * stack([self.p_layer] * sh.cols)
+        mine = ones((self.row_i >> 3) == x)
+        chip = j // 2
+        low = ones(iota((layer, layer), 1) < iota((layer, layer), 0))
+        seg_tri = ones((self.lane_tile == (self.r >> log2(sh.width))) & (self.r < self.l))
+        seg_full = ones(self.lane_tile == (self.r >> log2(sh.width)))
+        over = jnp.zeros((1, 1), F32)
+        for dc in range(sh.chips):
+            c = (chip + dc) % sh.chips
+            v = jnp.zeros((layer, n), F32)
+            for k in range(sh.cols):
+                v = jnp.maximum(v, reads[k * layer : (k + 1) * layer] * jnp.where(k // 2 == c, 1.0, 0.0))
+            v = v * mine
+            if dc == 0:
+                pos = mm(v, seg_tri) + mm(low, mm(v, seg_full))
+                pos = jnp.minimum(pos, CAP_R - 1.0)
+                continue
+            v = v * ones(self.row_tile == j)
+            rows, lanes, counts, starts, _ = self.enumerate(v, EIGHT)
+            line = mt(jnp.ones((EIGHT, n), F32), lanes * mm(rows, self.slot_layer))
+            tab[0:1, (dc - 1) * EIGHT : dc * EIGHT] = line[0:1].astype(I32)
+            over = over + total_over(counts, starts, CAP_R)
+        self.left_1 = jnp.where(
+            self.row_tile == j,
+            self.slot_layer,
+            jnp.where(
+                self.row_tile // 2 == chip,
+                sh.slots + self.slot_layer,
+                sh.others + self.row_tile.astype(F32) * CAP_R + pos,
+            ),
+        )
+        return over
+
+    def team_lists(self, tab):
+        sh, x, z, j, layer, n = self.sh, self.x, self.z, self.j, self.sh.layer, self.sh.nblk
+        a, b = iota((layer, layer), 0), iota((layer, layer), 1)
+        eye = ones(a == b)
+        turned = {"H": tm(self.p_layer, eye), "P": tm(self.f_layer, eye)}
+        lane_x = iota((n, layer), 1) >> 3
+        live = {"H": self.hm, "P": self.pm}
+        k_layer = self.r // layer
+        over = jnp.zeros((1, 1), F32)
+        self.pos = {}
+        for which, (kind, cap_z, cap) in enumerate((("H", CAP_H_Z, CAP_H), ("P", CAP_P_Z, CAP_P))):
+            pos_z = self.position(ones(mm(turned[kind], self.p_layer) > 0.5) * live[kind], self.low_layer)
+            far = (sh.team * sh.slots + k_layer * cap_z).astype(F32) + jnp.minimum(pos_z, cap_z - 1.0)
+            payload = jnp.where(k_layer == z, self.near[kind], far)
+            by_x = stack([turned[kind] * ones(lane_x == xd) for xd in range(sh.inner)])
+            needs = []
+            if kind == "H":
+                made = [
+                    ones(mm(by_x, self.outputs[c * layer : (c + 1) * layer]) > 0.5) for c in range(sh.cols)
+                ]
+            else:
+                one = ones(mm(by_x, self.p_layer) > 0.5)
+                made = [one * ones((iota((sh.inner * n, n), 1) >> log2(sh.width)) == c) for c in range(sh.cols)]
+            for xd in range(sh.inner):
+                for c in range(sh.cols):
+                    needs.append(made[c][xd * n : (xd + 1) * n] * live[kind])
+            all_needs = stack(needs)
+            lane_pos = mm(all_needs, self.up)
+            counts = stack([mt(jnp.ones((LIST, n), F32), v) for v in needs])
+            starts = mm(counts, self.up)
+            over = over + total_over(counts, starts, cap)
+            at = (iota((sh.team * LIST, n), 0) % LIST).astype(F32)
+            rows = ones((starts <= at) & (at < starts + counts))
+            local = mm(rows * (at - starts + 1.0), self.full)
+            marked = all_needs * (lane_pos + 1.0)
+            found = stack(
+                [
+                    mm(rows[t * LIST : (t + 1) * LIST], marked[t * n : (t + 1) * n])
+                    for t in range(sh.team)
+                ]
+            )
+            picked = jnp.where((found == local) & (local > 0.5), mm(rows, payload), 0.0)
+            line = mt(jnp.ones((EIGHT, n), F32), picked)
+            tab[which : which + 1, 0 : sh.team * LIST] = line[0:1].astype(I32)
+            me = x * sh.cols + j
+            mine = jnp.zeros((n, n), F32)
+            for t in range(sh.team):
+                mine = mine + needs[t] * jnp.where(me == t, 1.0, 0.0)
+            self.pos[kind] = jnp.minimum(self.position(mine, self.low), cap - 1.0)
+        return over
+
+    def products(self, pw, p_count, tab):
+        sh, x, z, j, layer, n = self.sh, self.x, self.z, self.j, self.sh.layer, self.sh.nblk
+        v = jnp.zeros((layer, n), F32)
+        for c in range(sh.cols):
+            v = v + self.remote_f[c * layer : (c + 1) * layer] * jnp.where(c == j, 1.0, 0.0)
+        v = v * ones((self.row_i >> 3) == x)
+        extra_rows, extra_cols, counts, starts, lane_pos = self.enumerate(v, EIGHT)
+        over = total_over(counts, starts, CAP_V)
+        low = ones(iota((layer, layer), 1) < iota((layer, layer), 0))
+        pos_v = jnp.minimum(lane_pos + mm(low, mm(v, self.full)), CAP_V - 1.0)
+        s0, s1 = iota((LIST, n), 0), iota((LIST, n), 1)
+        u0, u1 = iota((LIST, layer), 0), iota((LIST, layer), 1)
+        row_of = jnp.full((LIST, layer), -1, I32)
+        col_of = jnp.full((LIST, n), -1, I32)
+        for s in range(sh.slots):
+            live = s < p_count[0, 0]
+            row_of = jnp.where((u0 == s) & live, pw[0, s] - z * layer, row_of)
+            col_of = jnp.where((s0 == s) & live, pw[1, s], col_of)
+        own_rows, own_cols = ones(row_of == u1), ones(col_of == s1)
+        left_2 = jnp.where(self.row_tile == j, self.slot_layer, sh.slots + pos_v)
+        for step in range(2):
+            if step == 0:
+                oh_row, oh_col = stack([own_rows, extra_rows]), stack([own_cols, extra_cols])
+                left, right, from_left, kind, cap, count = self.p_layer, self.hm, self.left_1, "H", CAP_1, LIST_1
+            else:
+                oh_row, oh_col = own_rows, own_cols
+                left, right, from_left, kind, cap, count = self.f_layer, self.pm, left_2, "P", CAP_2, LIST
+            w = mm(oh_row, left) * mt(oh_col, right)
+            rows, lanes, counts, starts, _ = self.enumerate(w, count)
+            over = over + total_over(counts, starts, cap)
+            k = w.shape[0]
+            at = iota((count, k), 0).astype(F32)
+            eight = jnp.ones((EIGHT, n), F32)
+            lines = (
+                mt(eight, lanes * mm(rows, mm(oh_row, from_left * left))),
+                mt(eight, lanes * mm(rows, mt(oh_col, self.pos[kind]))),
+                mt(jnp.ones((EIGHT, k), F32), rows * ones(at > starts)),
+                jnp.where(counts > 0.5, jnp.minimum(starts + counts - 1.0, cap), 1.0 * cap),
+            )
+            for q, line in enumerate(lines):
+                size = line.shape[1]
+                tab[2 + step : 3 + step, 32 * q : 32 * q + size] = line[0:1].astype(I32)
+        return over
+
+
+def sparse_products(
+    sh, p_ref, h_ref, pw, pc, hw, hc, ph_out, php_out, e_out, over_out,
+    message, messages, near_h, near_p, store_h, store_p, prow, pack_r, pack_hz, pack_pz, pack_h, pack_p,
+    land_h, land_p, terms_1, terms_2, fstore, tabv_z, tabv_r, tabv, tab_z, tab_r, tab, emsg, emsgs,
+    m_send, m_recv, s_send, s_recv, p_send, p_fwd, p_recv, z_send, z_recv,
+    t_send, t_recv, e_send, e_recv, t_copy,
+):
+    i, j = lax.axis_index("row"), lax.axis_index("col")
+    x, z = i % sh.inner, i // sh.inner
+    me = i * sh.cols + j
+    chip, core = j // 2, j % 2
+    mate = (i, chip * 2 + 1 - core)
+    team = x * sh.cols + j
+    slots, strip, size = sh.slots, sh.strip, sh.size
+    all_but_me = sh.devices - 1
+
+    def device(d):
+        t = (me + d) % sh.devices
+        return (t // sh.cols, t % sh.cols)
+
+    def member(d):
+        q = (team + d) % sh.team
+        return q, (z * sh.inner + q // sh.cols, q % sh.cols)
+
+    def in_strip(q):
+        return pl.ds(pl.multiple_of(q * strip, strip), strip)
+
+    lane = iota((1, 128), 1)
+    packed = jnp.zeros((1, 128), F32)
+    for where, count, scale in ((pw, pc, 1.0), (hw, hc, 16.0)):
+        for s in range(slots):
+            at = (where[0, s] - i * TILE) * sh.width + where[1, s] - j * sh.width
+            packed = packed + jnp.where((lane == at) & (s < count[0, 0]), scale * (s + 1), 0.0)
+    message[0] = packed
+    messages[me] = packed
+
+    barrier = pltpu.get_barrier_semaphore()
+
+    @pl.loop(1, sh.devices)
+    def _(d):
+        pl.semaphore_signal(barrier, inc=1, device_id=device(d), device_id_type=MESH)
+
+    for s in range(slots):
+        near_h[team * slots + s] = h_ref[s, in_strip(team), :]
+        near_p[team * slots + s] = p_ref[s, in_strip(team), :]
+        prow[s] = p_ref[s]
+    pl.semaphore_wait(barrier, all_but_me)
+
+    def tell(d):
+        return remote(message.at[pl.ds(0, 1)], messages.at[pl.ds(me, 1)], m_send, m_recv, device(d))
+
+    @pl.loop(1, sh.devices)
+    def _(d):
+        tell(d).start()
+
+    def strips(d, which):
+        q, dev = member(d)
+        ref, near = ((h_ref, near_h), (p_ref, near_p))[which]
+        return remote(
+            ref.at[:, in_strip(q), :], near.at[pl.ds(team * slots, slots)],
+            s_send.at[which, d], s_recv.at[which, team], dev,
+        )
+
+    def strips_in(d, which):
+        q, dev = member(d)
+        ref, near = ((h_ref, near_h), (p_ref, near_p))[which]
+        return remote(
+            ref.at[:, in_strip(q), :], near.at[pl.ds(q * slots, slots)],
+            s_send.at[which, d], s_recv.at[which, q], dev,
+        )
+
+    for which in range(2):
+        for d in range(1, sh.team):
+            strips(d, which).start()
+
+    def other(dc):
+        c = (chip + dc) % sh.chips
+        return c, c * 2 + core
+
+    p_mate = remote(p_ref, prow.at[pl.ds(slots, slots)], p_send.at[0], p_recv.at[sh.cols], mate)
+    p_mate.start()
+
+    def p_block(col):
+        return prow.at[pl.ds(sh.others + col * CAP_R, CAP_R)]
+
+    def p_out(dc):
+        return remote(pack_r.at[dc - 1], p_block(j), p_send.at[dc], p_recv.at[j], (i, other(dc)[1]))
+
+    def p_in(dc):
+        col = other(dc)[1]
+        return remote(pack_r.at[dc - 1], p_block(col), p_send.at[dc], p_recv.at[col], (i, col))
+
+    def p_forward(dc):
+        col = other(dc)[1]
+        return remote(p_block(col), p_block(col), p_fwd.at[dc], p_recv.at[col], mate)
+
+    def p_forward_in(dc):
+        col = other(dc)[0] * 2 + 1 - core
+        return remote(p_block(col), p_block(col), p_fwd.at[dc], p_recv.at[col], mate)
+
+    def bulk(ref, sem):
+        part = ref.at[pl.ds(0, all_but_me)]
+        return pltpu.make_async_copy(part, part, sem)
+
+    bulk(messages, m_recv).wait()
+    lists = Lists(sh, x, z, j, messages[:, 0, :])
+
+    def publish(source, target, which):
+        copy = pltpu.make_async_copy(source, target, t_copy.at[which])
+        copy.start()
+        copy.wait()
+
+    def entry(ref, table, row, lane):
+        return ref[jnp.minimum(jnp.maximum(table[row, lane], 0), ref.shape[0] - 1)]
+
+    over = lists.across(tabv_z)
+    publish(tabv_z, tab_z, 0)
+
+    kinds = (
+        (store_h, pack_hz, pack_h, land_h, CAP_H_Z, CAP_H, near_h),
+        (store_p, pack_pz, pack_p, land_p, CAP_P_Z, CAP_P, near_p),
+    )
+
+    def zone(which, layer):
+        store, cap = kinds[which][0], kinds[which][4]
+        return store.at[pl.ds(sh.team * slots + layer * cap, cap)]
+
+    def across(which, dz):
+        pack = kinds[which][1]
+        zd = (z + dz) % sh.outer
+        return remote(
+            pack.at[dz - 1], zone(which, z), z_send.at[which, dz], z_recv.at[which, z],
+            (zd * sh.inner + x, j),
+        )
+
+    def across_in(which, dz):
+        pack = kinds[which][1]
+        zs = (z + dz) % sh.outer
+        return remote(
+            pack.at[dz - 1], zone(which, zs), z_send.at[which, dz], z_recv.at[which, zs],
+            (zs * sh.inner + x, j),
+        )
+
+    for which in range(2):
+        store, pack, _, _, cap, _, near = kinds[which]
+        for d in range(1, sh.team):
+            strips_in(d, which).wait_recv()
+        for dz in range(1, sh.outer):
+            for k in range(cap):
+                pack[dz - 1, k] = entry(near, tab_z, which, (dz - 1) * LIST_Z + k)
+        for dz in range(1, sh.outer):
+            across(which, dz).start()
+        store[0 : sh.team * slots] = near[...]
+
+    over = over + lists.row_lists(tabv_r)
+    publish(tabv_r, tab_r, 1)
+    for dc in range(1, sh.chips):
+        for k in range(CAP_R):
+            pack_r[dc - 1, k] = entry(p_ref, tab_r, 0, (dc - 1) * EIGHT + k)
+    for dc in range(1, sh.chips):
+        p_out(dc).start()
+
+    over = over + lists.team_lists(tabv)
+    over = over + lists.products(pw, pc, tabv)
+    publish(tabv, tab, 2)
+
+    def part(which, d):
+        pack, land = kinds[which][2], kinds[which][3]
+        _, dev = member(d)
+        return remote(
+            pack.at[d - 1], land.at[:, in_strip(team), :], t_send.at[which, d], t_recv.at[which, team], dev
+        )
+
+    def part_in(which, d):
+        pack, land = kinds[which][2], kinds[which][3]
+        q, dev = member(d)
+        return remote(
+            pack.at[d - 1], land.at[:, in_strip(q), :], t_send.at[which, d], t_recv.at[which, q], dev
+        )
+
+    for which in range(2):
+        store, _, pack, land, _, cap, _ = kinds[which]
+        for dz in range(1, sh.outer):
+            across_in(which, dz).wait_recv()
+
+        @pl.loop(1, sh.team)
+        def _(d):
+            q, _ = member(d)
+            for k in range(cap):
+                pack[d - 1, k] = entry(store, tab, which, q * LIST + k)
+
+        for d in range(1, sh.team):
+            part(which, d).start()
+        for k in range(cap):
+            land[k, in_strip(team), :] = entry(store, tab, which, team * LIST + k)
+
+    def multiply(step, left, right, terms, cap):
+        row = 2 + step
+        acc = None
+        for k in range(cap):
+            d = jnp.dot(entry(left, tab, row, k), entry(right, tab, row, 32 + k), preferred_element_type=F32)
+            acc = d if acc is None else d + acc * tab[row, 64 + k].astype(F32)
+            terms[k] = acc
+        terms[cap] = jnp.zeros((size, size), F32)
+
+    for dc in range(1, sh.chips):
+        p_in(dc).wait_recv()
+        p_forward(dc).start()
+    p_mate.wait_recv()
+    for dc in range(1, sh.chips):
+        p_forward_in(dc).wait_recv()
+    for d in range(1, sh.team):
+        part_in(0, d).wait_recv()
+    multiply(0, prow, land_h, terms_1, CAP_1)
+    trace = jnp.zeros((size, size), F32)
+    for s in range(slots):
+        value = entry(terms_1, tab, 2, 96 + s)
+        trace = trace + value * jnp.where(pw[0, s] == pw[1, s], 1.0, 0.0)
+        rounded = value.astype(BF16)
+        fstore[s] = rounded
+        ph_out[s] = rounded
+
+    for k in range(CAP_V):
+        fstore[slots + k] = entry(terms_1, tab, 2, 96 + LIST + k).astype(BF16)
+
+    diagonal = iota((size, size), 0) == iota((size, size), 1)
+    emsg[0, 0] = jnp.sum(jnp.where(diagonal, trace, 0.0), axis=0, keepdims=True)
+    emsg[0, 1] = over + jnp.zeros((1, 128), F32)
+    emsgs[me] = emsg[0]
+
+    def tell_energy(d):
+        return remote(emsg.at[pl.ds(0, 1)], emsgs.at[pl.ds(me, 1)], e_send, e_recv, device(d))
+
+    @pl.loop(1, sh.devices)
+    def _(d):
+        tell_energy(d).start()
+
+    for d in range(1, sh.team):
+        part_in(1, d).wait_recv()
+    multiply(1, fstore, land_p, terms_2, CAP_2)
+    for s in range(slots):
+        php_out[s] = entry(terms_2, tab, 3, 96 + s).astype(BF16)
+
+    bulk(emsgs, e_recv).wait()
+    e_out[0, 0] = jnp.sum(jnp.sum(emsgs[:, 0], axis=0))
+    over_out[0, 0] = jnp.sum(jnp.sum(emsgs[:, 1], axis=0))
+
+    bulk(messages, m_send).wait()
+    bulk(emsgs, e_send).wait()
+    for which in range(2):
+        for d in range(1, sh.team):
+            strips(d, which).wait_send()
+            part(which, d).wait_send()
+        for dz in range(1, sh.outer):
+            across(which, dz).wait_send()
+    p_mate.wait_send()
+    for dc in range(1, sh.chips):
+        p_out(dc).wait_send()
+        p_forward(dc).wait_send()
+
+
+def sparse_path(sh, p_values, p_where, p_count, h_values, h_where, h_count):
+    slots, size, strip = sh.slots, sh.size, sh.strip
+    block, piece = (size, size), (strip, size)
+    bf = lambda *shape: pltpu.VMEM(shape, BF16)
+    f32 = lambda *shape: pltpu.VMEM(shape, F32)
+    dma = pltpu.SemaphoreType.DMA
+    near = sh.team * slots
+    away = max(sh.outer - 1, 1)
+    chips = max(sh.chips - 1, 1)
+    tile = jax.ShapeDtypeStruct((slots,) + block, BF16)
+    scalar = jax.ShapeDtypeStruct((1, 1), F32)
+    return pl.pallas_call(
+        functools.partial(sparse_products, sh),
+        out_shape=[tile, tile, scalar, scalar],
+        in_specs=[VMEM, VMEM, SMEM, SMEM, SMEM, SMEM],
+        out_specs=[VMEM, VMEM, SMEM, SMEM],
+        scratch_shapes=[
+            f32(1, 1, 128),
+            f32(sh.devices, 1, 128),
+            bf(near, *piece),
+            bf(near, *piece),
+            bf(near + sh.outer * CAP_H_Z, *piece),
+            bf(near + sh.outer * CAP_P_Z, *piece),
+            bf(sh.others + sh.cols * CAP_R, *block),
+            bf(chips, CAP_R, *block),
+            bf(away, CAP_H_Z, *piece),
+            bf(away, CAP_P_Z, *piece),
+            bf(sh.team, CAP_H, *piece),
+            bf(sh.team, CAP_P, *piece),
+            bf(CAP_H, *block),
+            bf(CAP_P, *block),
+            f32(CAP_1 + 1, *block),
+            f32(CAP_2 + 1, *block),
+            bf(slots + CAP_V, *block),
+            pltpu.VMEM((8, 128), I32),
+            pltpu.VMEM((8, 128), I32),
+            pltpu.VMEM((8, 128), I32),
+            pltpu.SMEM((8, 128), I32),
+            pltpu.SMEM((8, 128), I32),
+            pltpu.SMEM((8, 128), I32),
+            f32(1, 2, 1, 128),
+            f32(sh.devices, 2, 1, 128),
+            dma, dma,
+            dma((2, sh.team)), dma((2, sh.team)),
+            dma((sh.chips,)), dma((sh.chips,)), dma((sh.cols + 1,)),
+            dma((2, sh.outer)), dma((2, sh.outer)),
+            dma((2, sh.team)), dma((2, sh.team)),
+            dma, dma, dma((3,)),
+        ],
+        compiler_params=pltpu.CompilerParams(collective_id=2, has_side_effects=True, vmem_limit_bytes=24 << 20),
+        name="sparse_products",
+    )(p_values, h_values, p_where.T, p_count, h_where.T, h_count)
+
+
+def per_device(rows, cols, *args):
+    slots, size, _ = args[0].shape
+    sh = Shape(rows, cols, slots, size)
+    if not sh.fits():
+        return dense_path(rows, cols, *args)
+    ph, php, energy, over = sparse_path(sh, *args)
+    return lax.cond(
+        over[0, 0] > 0.0,
+        lambda: dense_path(rows, cols, *args),
+        lambda: (ph, php, energy[0, 0]),
+    )
+
+
 def solution(mesh):
     placed = (
         P("row", "col", None),

time: 96.6 us -> 47.6 us (0.49)
  Pallas kernels: 92.9 us -> 40.5 us
  between operations: 1.95 us -> 4.33 us
  local copies, waits for them, and re-layouts: 1.45 us -> 2.51 us
    pallas_call x4 -> x1, Pallas kernels: 92.9 us -> 40.5 us  [sparse_path(): pl.pallas_call(functools.partial(sparse_products, sh), out_shape=[tile, t...]
    unnamed x0 -> x2, local copies, waits for them, and re-layouts: none -> 2.51 us
where the time goes in v2:
time: 47.6 us; the launch traced here: 47.4 us
  Pallas kernels  40.5 us (85%)
  between operations  4.33 us (9%)
  local copies, waits for them, and re-layouts  2.51 us (5%)
    pallas_call x1, Pallas kernels, sparse_path(): pl.pallas_call(functools.partial(sparse_products, sh), out_shape=[tile, t...  40.5 us
    unnamed x2, local copies, waits for them, and re-layouts  2.51 us

profile of v2, /device:TPU:0, one launch (start us, length us, event | category | flops | bytes accessed | tf_op | source)
XLA Modules:
  0.0 47.4 jit_solution(2929970816113678697)
XLA Ops:
  1.9 40.5 %sparse_products.1 = (bf16[12,128,128]{2,1,0:T(8,128)(2,1)}, bf16[12,128,128]{2,1,0:T(8,128)(2,1)S(1)}, f32[1,1]{1,0:T(1,128)}, f32[1,1]{1,0:T(1,128)}) custom-call(bf16[12,128,128]{2,1,0:T(8,128)(2,1)} %p_ref.1, bf16[12,128,128]{2,1,0:T(8,128)(2,1)} %h_ref.1, s32[2,12]{1,0:T(2,128)} %bitcast.22, s32[1,1]{1,0:T(1,128)S(6)} %copy.18.pc, s32[2,12]{1,0:T(2,128)} %bitcast.23, ...), custom_call_target="tpu_custom_call" | custom-call | tf_op jit(solution)/shard_map/sparse_products/pallas_call | solution.py:1032
  43.2 1.8 %copy.20 = bf16[12,128,128]{2,1,0:T(8,128)(2,1)} copy(bf16[12,128,128]{2,1,0:T(8,128)(2,1)} %get-tuple-element.67) | data formatting | bytes 786432
  44.9 0.7 %copy.21 = bf16[12,128,128]{2,1,0:T(8,128)(2,1)} copy(bf16[12,128,128]{2,1,0:T(8,128)(2,1)S(1)} %get-tuple-element.68) | data formatting | bytes 786432
  (1 shorter events, 0.0 us)

commit v3 on v2

--- a/solution.py
+++ b/solution.py
@@ -553,6 +553,7 @@
             both = both + jnp.where((l >> lw) == c, spread[c * n : (c + 1) * n], 0.0)
         hs = jnp.floor(both * (1.0 / 16.0))
         ps = both - 16.0 * hs
+        self.pos = {}
         self.pm, self.hm = ones(ps > 0.5), ones(hs > 0.5)
         self.fm = self.pm * ones(mm(self.pm, self.hm) > 0.5)
         self.up, self.low = ones(r < l), ones(l < r)
@@ -661,55 +662,53 @@
         )
         return over
 
-    def team_lists(self, tab):
+    def team_lists(self, which, tab):
         sh, x, z, j, layer, n = self.sh, self.x, self.z, self.j, self.sh.layer, self.sh.nblk
         a, b = iota((layer, layer), 0), iota((layer, layer), 1)
-        eye = ones(a == b)
-        turned = {"H": tm(self.p_layer, eye), "P": tm(self.f_layer, eye)}
+        turn = lambda m: tm(m, ones(a == b))
+        kind, cap_z, cap = (("H", CAP_H_Z, CAP_H), ("P", CAP_P_Z, CAP_P))[which]
+        turned = turn(self.p_layer if kind == "H" else self.f_layer)
+        live = self.hm if kind == "H" else self.pm
         lane_x = iota((n, layer), 1) >> 3
-        live = {"H": self.hm, "P": self.pm}
         k_layer = self.r // layer
-        over = jnp.zeros((1, 1), F32)
-        self.pos = {}
-        for which, (kind, cap_z, cap) in enumerate((("H", CAP_H_Z, CAP_H), ("P", CAP_P_Z, CAP_P))):
-            pos_z = self.position(ones(mm(turned[kind], self.p_layer) > 0.5) * live[kind], self.low_layer)
-            far = (sh.team * sh.slots + k_layer * cap_z).astype(F32) + jnp.minimum(pos_z, cap_z - 1.0)
-            payload = jnp.where(k_layer == z, self.near[kind], far)
-            by_x = stack([turned[kind] * ones(lane_x == xd) for xd in range(sh.inner)])
-            needs = []
-            if kind == "H":
-                made = [
-                    ones(mm(by_x, self.outputs[c * layer : (c + 1) * layer]) > 0.5) for c in range(sh.cols)
-                ]
-            else:
-                one = ones(mm(by_x, self.p_layer) > 0.5)
-                made = [one * ones((iota((sh.inner * n, n), 1) >> log2(sh.width)) == c) for c in range(sh.cols)]
-            for xd in range(sh.inner):
-                for c in range(sh.cols):
-                    needs.append(made[c][xd * n : (xd + 1) * n] * live[kind])
-            all_needs = stack(needs)
-            lane_pos = mm(all_needs, self.up)
-            counts = stack([mt(jnp.ones((LIST, n), F32), v) for v in needs])
-            starts = mm(counts, self.up)
-            over = over + total_over(counts, starts, cap)
-            at = (iota((sh.team * LIST, n), 0) % LIST).astype(F32)
-            rows = ones((starts <= at) & (at < starts + counts))
-            local = mm(rows * (at - starts + 1.0), self.full)
-            marked = all_needs * (lane_pos + 1.0)
-            found = stack(
-                [
-                    mm(rows[t * LIST : (t + 1) * LIST], marked[t * n : (t + 1) * n])
-                    for t in range(sh.team)
-                ]
-            )
-            picked = jnp.where((found == local) & (local > 0.5), mm(rows, payload), 0.0)
-            line = mt(jnp.ones((EIGHT, n), F32), picked)
-            tab[which : which + 1, 0 : sh.team * LIST] = line[0:1].astype(I32)
-            me = x * sh.cols + j
-            mine = jnp.zeros((n, n), F32)
-            for t in range(sh.team):
-                mine = mine + needs[t] * jnp.where(me == t, 1.0, 0.0)
-            self.pos[kind] = jnp.minimum(self.position(mine, self.low), cap - 1.0)
+        pos_z = self.position(ones(mm(turned, self.p_layer) > 0.5) * live, self.low_layer)
+        far = (sh.team * sh.slots + k_layer * cap_z).astype(F32) + jnp.minimum(pos_z, cap_z - 1.0)
+        payload = jnp.where(k_layer == z, self.near[kind], far)
+        by_x = stack([turned * ones(lane_x == xd) for xd in range(sh.inner)])
+        needs = []
+        if kind == "H":
+            made = [
+                ones(mm(by_x, self.outputs[c * layer : (c + 1) * layer]) > 0.5) for c in range(sh.cols)
+            ]
+        else:
+            one = ones(mm(by_x, self.p_layer) > 0.5)
+            made = [one * ones((iota((sh.inner * n, n), 1) >> log2(sh.width)) == c) for c in range(sh.cols)]
+        for xd in range(sh.inner):
+            for c in range(sh.cols):
+                needs.append(made[c][xd * n : (xd + 1) * n] * live)
+        all_needs = stack(needs)
+        lane_pos = mm(all_needs, self.up)
+        counts = stack([mt(jnp.ones((LIST, n), F32), v) for v in needs])
+        starts = mm(counts, self.up)
+        over = total_over(counts, starts, cap)
+        at = (iota((sh.team * LIST, n), 0) % LIST).astype(F32)
+        rows = ones((starts <= at) & (at < starts + counts))
+        local = mm(rows * (at - starts + 1.0), self.full)
+        marked = all_needs * (lane_pos + 1.0)
+        found = stack(
+            [
+                mm(rows[t * LIST : (t + 1) * LIST], marked[t * n : (t + 1) * n])
+                for t in range(sh.team)
+            ]
+        )
+        picked = jnp.where((found == local) & (local > 0.5), mm(rows, payload), 0.0)
+        line = mt(jnp.ones((EIGHT, n), F32), picked)
+        tab[0:1, 0 : sh.team * LIST] = line[0:1].astype(I32)
+        me = x * sh.cols + j
+        mine = jnp.zeros((n, n), F32)
+        for t in range(sh.team):
+            mine = mine + needs[t] * jnp.where(me == t, 1.0, 0.0)
+        self.pos[kind] = jnp.minimum(self.position(mine, self.low), cap - 1.0)
         return over
 
     def products(self, pw, p_count, tab):
@@ -758,11 +757,12 @@
 
 
 def sparse_products(
-    sh, p_ref, h_ref, pw, pc, hw, hc, ph_out, php_out, e_out, over_out,
+    sh, p_hbm, h_hbm, pw_hbm, pc_hbm, hw_hbm, hc_hbm, out, e_out, over_out,
+    p_ref, h_ref, pw, pc, hw, hc,
     message, messages, near_h, near_p, store_h, store_p, prow, pack_r, pack_hz, pack_pz, pack_h, pack_p,
-    land_h, land_p, terms_1, terms_2, fstore, tabv_z, tabv_r, tabv, tab_z, tab_r, tab, emsg, emsgs,
+    land_h, land_p, terms_1, terms_2, fstore, tabv_z, tabv_r, tabv_h, tabv, tab_z, tab_r, tab_h, tab, emsg, emsgs,
     m_send, m_recv, s_send, s_recv, p_send, p_fwd, p_recv, z_send, z_recv,
-    t_send, t_recv, e_send, e_recv, t_copy,
+    t_send, t_recv, e_send, e_recv, t_copy, fetch,
 ):
     i, j = lax.axis_index("row"), lax.axis_index("col")
     x, z = i % sh.inner, i // sh.inner
@@ -784,6 +784,25 @@
     def in_strip(q):
         return pl.ds(pl.multiple_of(q * strip, strip), strip)
 
+    fetches = [
+        pltpu.make_async_copy(source, target, fetch.at[k])
+        for k, (source, target) in enumerate(
+            (
+                (pw_hbm, pw), (pc_hbm, pc), (hw_hbm, hw), (hc_hbm, hc),
+                (h_hbm, h_ref), (p_hbm, p_ref),
+            )
+        )
+    ]
+    for copy in fetches:
+        copy.start()
+    barrier = pltpu.get_barrier_semaphore()
+
+    @pl.loop(1, sh.devices)
+    def _(d):
+        pl.semaphore_signal(barrier, inc=1, device_id=device(d), device_id_type=MESH)
+
+    for copy in fetches[:4]:
+        copy.wait()
     lane = iota((1, 128), 1)
     packed = jnp.zeros((1, 128), F32)
     for where, count, scale in ((pw, pc, 1.0), (hw, hc, 16.0)):
@@ -792,13 +811,8 @@
             packed = packed + jnp.where((lane == at) & (s < count[0, 0]), scale * (s + 1), 0.0)
     message[0] = packed
     messages[me] = packed
-
-    barrier = pltpu.get_barrier_semaphore()
-
-    @pl.loop(1, sh.devices)
-    def _(d):
-        pl.semaphore_signal(barrier, inc=1, device_id=device(d), device_id_type=MESH)
-
+    for copy in fetches[4:]:
+        copy.wait()
     for s in range(slots):
         near_h[team * slots + s] = h_ref[s, in_strip(team), :]
         near_p[team * slots + s] = p_ref[s, in_strip(team), :]
@@ -872,12 +886,9 @@
     def entry(ref, table, row, lane):
         return ref[jnp.minimum(jnp.maximum(table[row, lane], 0), ref.shape[0] - 1)]
 
-    over = lists.across(tabv_z)
-    publish(tabv_z, tab_z, 0)
-
     kinds = (
-        (store_h, pack_hz, pack_h, land_h, CAP_H_Z, CAP_H, near_h),
-        (store_p, pack_pz, pack_p, land_p, CAP_P_Z, CAP_P, near_p),
+        (store_h, pack_hz, pack_h, land_h, CAP_H_Z, CAP_H, near_h, tab_h),
+        (store_p, pack_pz, pack_p, land_p, CAP_P_Z, CAP_P, near_p, tab),
     )
 
     def zone(which, layer):
@@ -900,8 +911,22 @@
             (zs * sh.inner + x, j),
         )
 
-    for which in range(2):
-        store, pack, _, _, cap, _, near = kinds[which]
+    def part(which, d):
+        pack, land = kinds[which][2], kinds[which][3]
+        _, dev = member(d)
+        return remote(
+            pack.at[d - 1], land.at[:, in_strip(team), :], t_send.at[which, d], t_recv.at[which, team], dev
+        )
+
+    def part_in(which, d):
+        pack, land = kinds[which][2], kinds[which][3]
+        q, dev = member(d)
+        return remote(
+            pack.at[d - 1], land.at[:, in_strip(q), :], t_send.at[which, d], t_recv.at[which, q], dev
+        )
+
+    def send_across(which):
+        store, pack, _, _, cap, _, near, _ = kinds[which]
         for d in range(1, sh.team):
             strips_in(d, which).wait_recv()
         for dz in range(1, sh.outer):
@@ -911,6 +936,25 @@
             across(which, dz).start()
         store[0 : sh.team * slots] = near[...]
 
+    def send_parts(which):
+        store, _, pack, land, _, cap, _, table = kinds[which]
+        for dz in range(1, sh.outer):
+            across_in(which, dz).wait_recv()
+
+        @pl.loop(1, sh.team)
+        def _(d):
+            q, _ = member(d)
+            for k in range(cap):
+                pack[d - 1, k] = entry(store, table, 0, q * LIST + k)
+
+        for d in range(1, sh.team):
+            part(which, d).start()
+        for k in range(cap):
+            land[k, in_strip(team), :] = entry(store, table, 0, team * LIST + k)
+
+    over = lists.across(tabv_z)
+    publish(tabv_z, tab_z, 0)
+    send_across(0)
     over = over + lists.row_lists(tabv_r)
     publish(tabv_r, tab_r, 1)
     for dc in range(1, sh.chips):
@@ -918,40 +962,17 @@
             pack_r[dc - 1, k] = entry(p_ref, tab_r, 0, (dc - 1) * EIGHT + k)
     for dc in range(1, sh.chips):
         p_out(dc).start()
-
-    over = over + lists.team_lists(tabv)
+    over = over + lists.team_lists(0, tabv_h)
+    publish(tabv_h, tab_h, 2)
+    send_across(1)
+    send_parts(0)
+    over = over + lists.team_lists(1, tabv)
     over = over + lists.products(pw, pc, tabv)
-    publish(tabv, tab, 2)
-
-    def part(which, d):
-        pack, land = kinds[which][2], kinds[which][3]
-        _, dev = member(d)
-        return remote(
-            pack.at[d - 1], land.at[:, in_strip(team), :], t_send.at[which, d], t_recv.at[which, team], dev
-        )
-
-    def part_in(which, d):
-        pack, land = kinds[which][2], kinds[which][3]
-        q, dev = member(d)
-        return remote(
-            pack.at[d - 1], land.at[:, in_strip(q), :], t_send.at[which, d], t_recv.at[which, q], dev
-        )
-
-    for which in range(2):
-        store, _, pack, land, _, cap, _ = kinds[which]
-        for dz in range(1, sh.outer):
-            across_in(which, dz).wait_recv()
-
-        @pl.loop(1, sh.team)
-        def _(d):
-            q, _ = member(d)
-            for k in range(cap):
-                pack[d - 1, k] = entry(store, tab, which, q * LIST + k)
-
-        for d in range(1, sh.team):
-            part(which, d).start()
-        for k in range(cap):
-            land[k, in_strip(team), :] = entry(store, tab, which, team * LIST + k)
+    publish(tabv, tab, 3)
+    for dc in range(1, sh.chips):
+        p_in(dc).wait_recv()
+        p_forward(dc).start()
+    send_parts(1)
 
     def multiply(step, left, right, terms, cap):
         row = 2 + step
@@ -962,9 +983,6 @@
             terms[k] = acc
         terms[cap] = jnp.zeros((size, size), F32)
 
-    for dc in range(1, sh.chips):
-        p_in(dc).wait_recv()
-        p_forward(dc).start()
     p_mate.wait_recv()
     for dc in range(1, sh.chips):
         p_forward_in(dc).wait_recv()
@@ -977,7 +995,7 @@
         trace = trace + value * jnp.where(pw[0, s] == pw[1, s], 1.0, 0.0)
         rounded = value.astype(BF16)
         fstore[s] = rounded
-        ph_out[s] = rounded
+        out[s] = rounded
 
     for k in range(CAP_V):
         fstore[slots + k] = entry(terms_1, tab, 2, 96 + LIST + k).astype(BF16)
@@ -998,7 +1016,7 @@
         part_in(1, d).wait_recv()
     multiply(1, fstore, land_p, terms_2, CAP_2)
     for s in range(slots):
-        php_out[s] = entry(terms_2, tab, 3, 96 + s).astype(BF16)
+        out[slots + s] = entry(terms_2, tab, 3, 96 + s).astype(BF16)
 
     bulk(emsgs, e_recv).wait()
     e_out[0, 0] = jnp.sum(jnp.sum(emsgs[:, 0], axis=0))
@@ -1027,14 +1045,19 @@
     near = sh.team * slots
     away = max(sh.outer - 1, 1)
     chips = max(sh.chips - 1, 1)
-    tile = jax.ShapeDtypeStruct((slots,) + block, BF16)
     scalar = jax.ShapeDtypeStruct((1, 1), F32)
     return pl.pallas_call(
         functools.partial(sparse_products, sh),
-        out_shape=[tile, tile, scalar, scalar],
-        in_specs=[VMEM, VMEM, SMEM, SMEM, SMEM, SMEM],
-        out_specs=[VMEM, VMEM, SMEM, SMEM],
+        out_shape=[jax.ShapeDtypeStruct((2 * slots,) + block, BF16), scalar, scalar],
+        in_specs=[ANY] * 6,
+        out_specs=[VMEM, SMEM, SMEM],
         scratch_shapes=[
+            bf(slots, *block),
+            bf(slots, *block),
+            pltpu.SMEM((2, slots), I32),
+            pltpu.SMEM((1, 1), I32),
+            pltpu.SMEM((2, slots), I32),
+            pltpu.SMEM((1, 1), I32),
             f32(1, 1, 128),
             f32(sh.devices, 1, 128),
             bf(near, *piece),
@@ -1055,6 +1078,8 @@
             pltpu.VMEM((8, 128), I32),
             pltpu.VMEM((8, 128), I32),
             pltpu.VMEM((8, 128), I32),
+            pltpu.VMEM((8, 128), I32),
+            pltpu.SMEM((8, 128), I32),
             pltpu.SMEM((8, 128), I32),
             pltpu.SMEM((8, 128), I32),
             pltpu.SMEM((8, 128), I32),
@@ -1065,11 +1090,34 @@
             dma((sh.chips,)), dma((sh.chips,)), dma((sh.cols + 1,)),
             dma((2, sh.outer)), dma((2, sh.outer)),
             dma((2, sh.team)), dma((2, sh.team)),
-            dma, dma, dma((3,)),
+            dma, dma, dma((4,)), dma((6,)),
         ],
         compiler_params=pltpu.CompilerParams(collective_id=2, has_side_effects=True, vmem_limit_bytes=24 << 20),
         name="sparse_products",
     )(p_values, h_values, p_where.T, p_count, h_where.T, h_count)
+
+
+def deliver(both):
+    def kernel(both_ref, first, second, sems):
+        slots = first.shape[0]
+        copies = [
+            pltpu.make_async_copy(both_ref.at[pl.ds(k * slots, slots)], ref, sems.at[k])
+            for k, ref in enumerate((first, second))
+        ]
+        for copy in copies:
+            copy.start()
+        for copy in copies:
+            copy.wait()
+
+    half = jax.ShapeDtypeStruct((both.shape[0] // 2,) + both.shape[1:], both.dtype)
+    return pl.pallas_call(
+        kernel,
+        out_shape=[half, half],
+        in_specs=[VMEM],
+        out_specs=[ANY, ANY],
+        scratch_shapes=[pltpu.SemaphoreType.DMA((2,))],
+        name="deliver",
+    )(both)
 
 
 def per_device(rows, cols, *args):
@@ -1077,11 +1125,11 @@
     sh = Shape(rows, cols, slots, size)
     if not sh.fits():
         return dense_path(rows, cols, *args)
-    ph, php, energy, over = sparse_path(sh, *args)
+    both, energy, over = sparse_path(sh, *args)
     return lax.cond(
         over[0, 0] > 0.0,
         lambda: dense_path(rows, cols, *args),
-        lambda: (ph, php, energy[0, 0]),
+        lambda: (*deliver(both), energy[0, 0]),
     )
 
 

time: 47.6 us -> 44.4 us (0.933)
  local copies, waits for them, and re-layouts: 2.51 us -> 0 us
  Pallas kernels: 40.5 us -> 39.9 us
    unnamed x2 -> x0, local copies, waits for them, and re-layouts: 2.51 us -> none
    pallas_call x1 -> x2, Pallas kernels: 40.5 us -> 39.9 us  [the longest x1 39 us: sparse_path(): pl.pallas_call(functools.partial(sparse_products, sh), out_shape=[jax.Sha...]
where the time goes in v3:
time: 44.4 us; the launch traced here: 44.2 us
  Pallas kernels  39.9 us (90%)
  between operations  4.33 us (10%)
    pallas_call x1, Pallas kernels, sparse_path(): pl.pallas_call(functools.partial(sparse_products, sh), out_shape=[jax.Sha...  39 us
    pallas_call x1, Pallas kernels, deliver(): pl.pallas_call(kernel, out_shape=[half, half], in_specs=[VMEM], out_specs...  0.89 us

profile of v3, /device:TPU:0, one launch (start us, length us, event | category | flops | bytes accessed | tf_op | source)
XLA Modules:
  0.0 44.2 jit_solution(15823912511977797806)
XLA Ops:
  1.9 39.0 %sparse_products.1 = (bf16[24,128,128]{2,1,0:T(8,128)(2,1)S(1)}, f32[1,1]{1,0:T(1,128)}, f32[1,1]{1,0:T(1,128)}) custom-call(bf16[12,128,128]{2,1,0:T(8,128)(2,1)} %p_hbm.1, bf16[12,128,128]{2,1,0:T(8,128)(2,1)} %h_hbm.1, s32[2,12]{1,0:T(2,128)} %bitcast.22, s32[1,1]{1,0:T(1,128)S(6)} %copy.16.pc_hbm, s32[2,12]{1,0:T(2,128)} %bitcast.23, s32[1,1]{1,0:T(1,128)S(6)} %copy.17.hc_hbm), custom_call_target="tpu_custom_call" | custom-call | tf_op jit(solution)/shard_map/sparse_products/pallas_call | solution.py:1049
  41.5 0.9 %conditional.1 = (bf16[12,128,128]{2,1,0:T(8,128)(2,1)}, bf16[12,128,128]{2,1,0:T(8,128)(2,1)}, f32[1,1]{1,0:T(1,128)}) conditional(s32[]{:T(128)} %bitcast.12, (bf16[24,128,128]{2,1,0:T(8,128)(2,1)S(1)}, f32[1,1]{1,0:T(1,128)}) %tuple.15, (s32[12,2]{0,1:T(2,128)}, s32[12,2]{0,1:T(2,128)}, s32[1,1]{1,0:T(1,128)}, s32[1,1]{1,0:T(1,128)}, ...), branch_computations={%region_0.0_spmd, %region_1.2_spmd} | conditional | bytes 1579024 | solution.py:1129
  41.5 0.9 %deliver.1 = (bf16[12,128,128]{2,1,0:T(8,128)(2,1)}, bf16[12,128,128]{2,1,0:T(8,128)(2,1)}) custom-call(bf16[24,128,128]{2,1,0:T(8,128)(2,1)S(1)} %get-tuple-element.16.both_ref), custom_call_target="tpu_custom_call" | custom-call | tf_op jit(solution)/shard_map/cond/branch_0_fun/deliver/pallas_call | solution.py:1113

commit v4 on v3

--- a/solution.py
+++ b/solution.py
@@ -459,7 +459,7 @@
 
 CAP_H_Z, CAP_P_Z = 17, 12
 CAP_H, CAP_P = 14, 9
-CAP_R, CAP_V = 7, 7
+CAP_R, CAP_V, CAP_D = 7, 7, 3
 CAP_1, CAP_2 = 18, 12
 LIST, LIST_Z, LIST_1, EIGHT = 16, 24, 24, 8
 F32, BF16, I32 = jnp.float32, jnp.bfloat16, jnp.int32
@@ -487,6 +487,17 @@
         self.chips = cols // 2
         self.others = 2 * slots
 
+    def trace_member(self, z, xd):
+        return xd * self.cols + (z * self.inner + xd) * TILE // self.width
+
+    def layer_at(self, z, t):
+        down = self.outer - 1 - t
+        return jnp.where(
+            z < self.outer // 2,
+            down - jnp.where(down <= z, 1, 0),
+            t + jnp.where(t >= z, 1, 0),
+        )
+
     def fits(self):
         return (
             power(self.rows)
@@ -494,7 +505,7 @@
             and self.cols >= 2
             and self.outer >= 2
             and self.nblk <= 64
-            and self.width * TILE <= 128
+            and TILE <= self.width <= 128 // TILE
             and self.slots <= 15
             and self.strip % 16 == 0
             and self.team * LIST <= 128
@@ -527,8 +538,8 @@
     return iota(shape, dim) // size
 
 
-def total_over(counts, starts, cap):
-    over = ones(starts + counts > cap + 0.5)
+def total_over(ends, cap):
+    over = ones(ends > cap + 0.5)
     return jnp.sum(jnp.sum(over, axis=0, keepdims=True), axis=1, keepdims=True)
 
 
@@ -556,7 +567,7 @@
         self.pos = {}
         self.pm, self.hm = ones(ps > 0.5), ones(hs > 0.5)
         self.fm = self.pm * ones(mm(self.pm, self.hm) > 0.5)
-        self.up, self.low = ones(r < l), ones(l < r)
+        self.up, self.low, self.up_to = ones(r < l), ones(l < r), ones(r <= l)
         self.low_layer = ones((l < r) & (l // layer == r // layer))
         self.full = jnp.ones((n, n), F32)
         self.r, self.l, self.lane_tile = r, l, l >> lw
@@ -573,15 +584,15 @@
         k, n = v.shape
         counts = mt(jnp.ones((count, n), F32), v)
         a, b = iota((k, k), 0), iota((k, k), 1)
-        starts = mm(counts, ones(a < b))
+        starts, ends = mm(counts, ones(a < b)), mm(counts, ones(a <= b))
         at = iota((count, k), 0).astype(F32)
-        rows = ones((starts <= at) & (at < starts + counts))
+        rows = ones((starts <= at) & (at < ends))
         local = mm(rows * (at - starts + 1.0), jnp.ones((k, n), F32))
         if lane_pos is None:
             lane_pos = mm(v, self.up)
         found = mm(rows, v * (lane_pos + 1.0))
         lanes = ones((found == local) & (local > 0.5))
-        return rows, lanes, counts, starts, lane_pos
+        return rows, lanes, starts, ends, lane_pos
 
     def position(self, v, low):
         return mm(v, self.up) + mm(low, mm(v, self.full))
@@ -594,7 +605,7 @@
         for kind, left, right in (("H", p_s, self.hm), ("P", f_s, self.pm)):
             live_kind, pay_kind = mm(self.sel, right), mm(self.sel, self.near[kind])
             for dz in range(1, sh.outer):
-                lhs.append(left * ones(i_layer == (z + dz) % sh.outer))
+                lhs.append(left * ones(i_layer == sh.layer_at(z, dz - 1)))
                 live.append(live_kind)
                 pay.append(pay_kind)
         v = ones(mm(stack(lhs), self.pm) > 0.5) * stack(live)
@@ -603,11 +614,12 @@
         a, b = iota((k, k), 0), iota((k, k), 1)
         counts = mt(jnp.ones((EIGHT, n), F32), v)
         starts = mm(counts, ones((a < b) & (a // layer == b // layer)))
+        ends = mm(counts, ones((a <= b) & (a // layer == b // layer)))
         t0 = iota((lists * LIST_Z, k), 0)
         at = (t0 % LIST_Z).astype(F32)
         rows = ones(
             (starts[0:1] <= at)
-            & (at < starts[0:1] + counts[0:1])
+            & (at < ends[0:1])
             & (t0 // LIST_Z == block_index((lists * LIST_Z, k), 1, layer))
         )
         local = mm(rows * (at - starts[0:1] + 1.0), jnp.ones((k, n), F32))
@@ -619,7 +631,7 @@
             tab[which : which + 1, 0:half] = line[0:1].astype(I32)
         lane_h = block_index((EIGHT, k), 1, layer) < sh.outer - 1
         cap = jnp.where(lane_h, 1.0 * CAP_H_Z, 1.0 * CAP_P_Z)
-        return total_over(counts - cap, starts, 0.0)
+        return total_over(ends - cap, 0.0)
 
     def row_lists(self, tab):
         sh, x, j, layer, n = self.sh, self.x, self.j, self.sh.layer, self.sh.nblk
@@ -647,10 +659,10 @@
                 pos = jnp.minimum(pos, CAP_R - 1.0)
                 continue
             v = v * ones(self.row_tile == j)
-            rows, lanes, counts, starts, _ = self.enumerate(v, EIGHT)
+            rows, lanes, starts, ends, _ = self.enumerate(v, EIGHT)
             line = mt(jnp.ones((EIGHT, n), F32), lanes * mm(rows, self.slot_layer))
             tab[0:1, (dc - 1) * EIGHT : dc * EIGHT] = line[0:1].astype(I32)
-            over = over + total_over(counts, starts, CAP_R)
+            over = over + total_over(ends, CAP_R)
         self.left_1 = jnp.where(
             self.row_tile == j,
             self.slot_layer,
@@ -689,10 +701,12 @@
         all_needs = stack(needs)
         lane_pos = mm(all_needs, self.up)
         counts = stack([mt(jnp.ones((LIST, n), F32), v) for v in needs])
-        starts = mm(counts, self.up)
-        over = total_over(counts, starts, cap)
+        starts, ends = mm(counts, self.up), mm(counts, self.up_to)
+        over = total_over(ends, cap)
+        if kind == "H":
+            over = over + self.trace_lists(payload, tab)
         at = (iota((sh.team * LIST, n), 0) % LIST).astype(F32)
-        rows = ones((starts <= at) & (at < starts + counts))
+        rows = ones((starts <= at) & (at < ends))
         local = mm(rows * (at - starts + 1.0), self.full)
         marked = all_needs * (lane_pos + 1.0)
         found = stack(
@@ -711,14 +725,36 @@
         self.pos[kind] = jnp.minimum(self.position(mine, self.low), cap - 1.0)
         return over
 
+    def trace_lists(self, payload, tab):
+        sh, n = self.sh, self.sh.nblk
+        eye = ones(self.r == self.l)
+        diagonal = jnp.sum(self.pm * eye, axis=0, keepdims=True)
+        every = tm(self.pm, eye) * self.hm * diagonal
+        eight = jnp.ones((EIGHT, n), F32)
+        over = jnp.zeros((1, 1), F32)
+        mine_rows, mine_lanes = jnp.zeros((EIGHT, n), F32), jnp.zeros((EIGHT, n), F32)
+        for xd in range(sh.inner):
+            v = every * ones((self.l >> 3) == self.z * sh.inner + xd)
+            rows, lanes, starts, ends, _ = self.enumerate(v, EIGHT)
+            over = over + total_over(ends, CAP_D)
+            line = mt(eight, lanes * mm(rows, payload))
+            tab[1:2, xd * EIGHT : (xd + 1) * EIGHT] = line[0:1].astype(I32)
+            here = jnp.where(self.x == xd, 1.0, 0.0)
+            mine_rows, mine_lanes = mine_rows + here * rows, mine_lanes + here * lanes
+        left = mm(mt(mine_lanes, self.sel), self.left_1 * self.p_layer) * mine_rows
+        for q, value in enumerate((left, mine_rows)):
+            line = mt(eight, value)
+            tab[2:3, 32 * q : 32 * q + EIGHT] = line[0:1].astype(I32)
+        return over
+
     def products(self, pw, p_count, tab):
         sh, x, z, j, layer, n = self.sh, self.x, self.z, self.j, self.sh.layer, self.sh.nblk
         v = jnp.zeros((layer, n), F32)
         for c in range(sh.cols):
             v = v + self.remote_f[c * layer : (c + 1) * layer] * jnp.where(c == j, 1.0, 0.0)
         v = v * ones((self.row_i >> 3) == x)
-        extra_rows, extra_cols, counts, starts, lane_pos = self.enumerate(v, EIGHT)
-        over = total_over(counts, starts, CAP_V)
+        extra_rows, extra_cols, starts, ends, lane_pos = self.enumerate(v, EIGHT)
+        over = total_over(ends, CAP_V)
         low = ones(iota((layer, layer), 1) < iota((layer, layer), 0))
         pos_v = jnp.minimum(lane_pos + mm(low, mm(v, self.full)), CAP_V - 1.0)
         s0, s1 = iota((LIST, n), 0), iota((LIST, n), 1)
@@ -739,8 +775,8 @@
                 oh_row, oh_col = own_rows, own_cols
                 left, right, from_left, kind, cap, count = self.f_layer, self.pm, left_2, "P", CAP_2, LIST
             w = mm(oh_row, left) * mt(oh_col, right)
-            rows, lanes, counts, starts, _ = self.enumerate(w, count)
-            over = over + total_over(counts, starts, cap)
+            rows, lanes, starts, ends, _ = self.enumerate(w, count)
+            over = over + total_over(ends, cap)
             k = w.shape[0]
             at = iota((count, k), 0).astype(F32)
             eight = jnp.ones((EIGHT, n), F32)
@@ -748,7 +784,7 @@
                 mt(eight, lanes * mm(rows, mm(oh_row, from_left * left))),
                 mt(eight, lanes * mm(rows, mt(oh_col, self.pos[kind]))),
                 mt(jnp.ones((EIGHT, k), F32), rows * ones(at > starts)),
-                jnp.where(counts > 0.5, jnp.minimum(starts + counts - 1.0, cap), 1.0 * cap),
+                jnp.where(ends > starts, jnp.minimum(ends - 1.0, cap), 1.0 * cap),
             )
             for q, line in enumerate(lines):
                 size = line.shape[1]
@@ -760,9 +796,9 @@
     sh, p_hbm, h_hbm, pw_hbm, pc_hbm, hw_hbm, hc_hbm, out, e_out, over_out,
     p_ref, h_ref, pw, pc, hw, hc,
     message, messages, near_h, near_p, store_h, store_p, prow, pack_r, pack_hz, pack_pz, pack_h, pack_p,
-    land_h, land_p, terms_1, terms_2, fstore, tabv_z, tabv_r, tabv_h, tabv, tab_z, tab_r, tab_h, tab, emsg, emsgs,
+    pack_d, land_d, land_h, land_p, terms_1, terms_2, fstore, tabv_z, tabv_r, tabv_h, tabv, tab_z, tab_r, tab_h, tab, emsg, emsgs,
     m_send, m_recv, s_send, s_recv, p_send, p_fwd, p_recv, z_send, z_recv,
-    t_send, t_recv, e_send, e_recv, t_copy, fetch,
+    t_send, t_recv, d_send, d_recv, e_send, e_recv, t_copy, fetch,
 ):
     i, j = lax.axis_index("row"), lax.axis_index("col")
     x, z = i % sh.inner, i // sh.inner
@@ -773,13 +809,23 @@
     slots, strip, size = sh.slots, sh.strip, sh.size
     all_but_me = sh.devices - 1
 
-    def device(d):
-        t = (me + d) % sh.devices
-        return (t // sh.cols, t % sh.cols)
-
     def member(d):
-        q = (team + d) % sh.team
-        return q, (z * sh.inner + q // sh.cols, q % sh.cols)
+        e = sh.team - d
+        qx = (x + e // sh.cols) % sh.inner
+        qj = (chip + (e // 2) % sh.chips) % sh.chips * 2 + (core + e % 2) % 2
+        return qx * sh.cols + qj, (z * sh.inner + qx, qj)
+
+    def for_others(act):
+        for t in range(sh.outer - 1):
+            zt = sh.layer_at(z, t)
+
+            @pl.loop(0, sh.team)
+            def _(q):
+                act((zt * sh.inner + q // sh.cols, q % sh.cols))
+
+        @pl.loop(1, sh.team)
+        def _(d):
+            act(member(d)[1])
 
     def in_strip(q):
         return pl.ds(pl.multiple_of(q * strip, strip), strip)
@@ -797,9 +843,7 @@
         copy.start()
     barrier = pltpu.get_barrier_semaphore()
 
-    @pl.loop(1, sh.devices)
-    def _(d):
-        pl.semaphore_signal(barrier, inc=1, device_id=device(d), device_id_type=MESH)
+    for_others(lambda dev: pl.semaphore_signal(barrier, inc=1, device_id=dev, device_id_type=MESH))
 
     for copy in fetches[:4]:
         copy.wait()
@@ -819,12 +863,10 @@
         prow[s] = p_ref[s]
     pl.semaphore_wait(barrier, all_but_me)
 
-    def tell(d):
-        return remote(message.at[pl.ds(0, 1)], messages.at[pl.ds(me, 1)], m_send, m_recv, device(d))
-
-    @pl.loop(1, sh.devices)
-    def _(d):
-        tell(d).start()
+    def tell(dev):
+        remote(message.at[pl.ds(0, 1)], messages.at[pl.ds(me, 1)], m_send, m_recv, dev).start()
+
+    for_others(tell)
 
     def strips(d, which):
         q, dev = member(d)
@@ -897,7 +939,7 @@
 
     def across(which, dz):
         pack = kinds[which][1]
-        zd = (z + dz) % sh.outer
+        zd = sh.layer_at(z, dz - 1)
         return remote(
             pack.at[dz - 1], zone(which, z), z_send.at[which, dz], z_recv.at[which, z],
             (zd * sh.inner + x, j),
@@ -905,7 +947,7 @@
 
     def across_in(which, dz):
         pack = kinds[which][1]
-        zs = (z + dz) % sh.outer
+        zs = sh.layer_at(z, dz - 1)
         return remote(
             pack.at[dz - 1], zone(which, zs), z_send.at[which, dz], z_recv.at[which, zs],
             (zs * sh.inner + x, j),
@@ -936,10 +978,36 @@
             across(which, dz).start()
         store[0 : sh.team * slots] = near[...]
 
+    def to_trace(xd):
+        return remote(
+            pack_d.at[xd], land_d.at[:, in_strip(team), :], d_send.at[xd], d_recv.at[team],
+            (z * sh.inner + xd, sh.trace_member(z, xd) % sh.cols),
+        )
+
+    def trace_in(d):
+        q, dev = member(d)
+        return remote(pack_d.at[0], land_d.at[:, in_strip(q), :], d_send.at[0], d_recv.at[q], dev)
+
+    def send_trace():
+        for xd in range(sh.inner):
+            for k in range(CAP_D):
+                pack_d[xd, k] = entry(store_h, tab_h, 1, xd * EIGHT + k)
+        for xd in range(sh.inner):
+            @pl.when(sh.trace_member(z, xd) != team)
+            def _():
+                to_trace(xd).start()
+
+            @pl.when(sh.trace_member(z, xd) == team)
+            def _():
+                for k in range(CAP_D):
+                    land_d[k, in_strip(team), :] = pack_d[xd, k]
+
     def send_parts(which):
         store, _, pack, land, _, cap, _, table = kinds[which]
         for dz in range(1, sh.outer):
             across_in(which, dz).wait_recv()
+        if which == 0:
+            send_trace()
 
         @pl.loop(1, sh.team)
         def _(d):
@@ -966,12 +1034,33 @@
     publish(tabv_h, tab_h, 2)
     send_across(1)
     send_parts(0)
+    for dc in range(1, sh.chips):
+        p_in(dc).wait_recv()
+        p_forward(dc).start()
     over = over + lists.team_lists(1, tabv)
     over = over + lists.products(pw, pc, tabv)
     publish(tabv, tab, 3)
+    p_mate.wait_recv()
     for dc in range(1, sh.chips):
-        p_in(dc).wait_recv()
-        p_forward(dc).start()
+        p_forward_in(dc).wait_recv()
+    emsg[0, 0] = jnp.zeros((1, 128), F32)
+
+    @pl.when(sh.trace_member(z, x) == team)
+    def _():
+        for d in range(1, sh.team):
+            trace_in(d).wait_recv()
+        for k in range(CAP_D):
+            part_of = entry(prow, tab_h, 2, k).astype(F32) * jnp.transpose(land_d[k].astype(F32))
+            total = jnp.sum(part_of, axis=0, keepdims=True)
+            emsg[0, 0] += total * tab_h[2, 32 + k].astype(F32)
+
+    emsg[0, 1] = over + jnp.zeros((1, 128), F32)
+    emsgs[me] = emsg[0]
+
+    def tell_energy(dev):
+        remote(emsg.at[pl.ds(0, 1)], emsgs.at[pl.ds(me, 1)], e_send, e_recv, dev).start()
+
+    for_others(tell_energy)
     send_parts(1)
 
     def multiply(step, left, right, terms, cap):
@@ -983,16 +1072,11 @@
             terms[k] = acc
         terms[cap] = jnp.zeros((size, size), F32)
 
-    p_mate.wait_recv()
-    for dc in range(1, sh.chips):
-        p_forward_in(dc).wait_recv()
     for d in range(1, sh.team):
         part_in(0, d).wait_recv()
     multiply(0, prow, land_h, terms_1, CAP_1)
-    trace = jnp.zeros((size, size), F32)
     for s in range(slots):
         value = entry(terms_1, tab, 2, 96 + s)
-        trace = trace + value * jnp.where(pw[0, s] == pw[1, s], 1.0, 0.0)
         rounded = value.astype(BF16)
         fstore[s] = rounded
         out[s] = rounded
@@ -1000,17 +1084,6 @@
     for k in range(CAP_V):
         fstore[slots + k] = entry(terms_1, tab, 2, 96 + LIST + k).astype(BF16)
 
-    diagonal = iota((size, size), 0) == iota((size, size), 1)
-    emsg[0, 0] = jnp.sum(jnp.where(diagonal, trace, 0.0), axis=0, keepdims=True)
-    emsg[0, 1] = over + jnp.zeros((1, 128), F32)
-    emsgs[me] = emsg[0]
-
-    def tell_energy(d):
-        return remote(emsg.at[pl.ds(0, 1)], emsgs.at[pl.ds(me, 1)], e_send, e_recv, device(d))
-
-    @pl.loop(1, sh.devices)
-    def _(d):
-        tell_energy(d).start()
 
     for d in range(1, sh.team):
         part_in(1, d).wait_recv()
@@ -1030,6 +1103,10 @@
             part(which, d).wait_send()
         for dz in range(1, sh.outer):
             across(which, dz).wait_send()
+    for xd in range(sh.inner):
+        @pl.when(sh.trace_member(z, xd) != team)
+        def _():
+            to_trace(xd).wait_send()
     p_mate.wait_send()
     for dc in range(1, sh.chips):
         p_out(dc).wait_send()
@@ -1070,6 +1147,8 @@
             bf(away, CAP_P_Z, *piece),
             bf(sh.team, CAP_H, *piece),
             bf(sh.team, CAP_P, *piece),
+            bf(sh.inner, CAP_D, *piece),
+            bf(CAP_D, *block),
             bf(CAP_H, *block),
             bf(CAP_P, *block),
             f32(CAP_1 + 1, *block),
@@ -1090,6 +1169,7 @@
             dma((sh.chips,)), dma((sh.chips,)), dma((sh.cols + 1,)),
             dma((2, sh.outer)), dma((2, sh.outer)),
             dma((2, sh.team)), dma((2, sh.team)),
+            dma((sh.inner,)), dma((sh.team,)),
             dma, dma, dma((4,)), dma((6,)),
         ],
         compiler_params=pltpu.CompilerParams(collective_id=2, has_side_effects=True, vmem_limit_bytes=24 << 20),

time: 44.4 us -> 41.6 us (0.937)
  Pallas kernels: 39.9 us -> 37.1 us
    pallas_call x1, Pallas kernels: 39 us -> 36.2 us  [sparse_path(): pl.pallas_call(functools.partial(sparse_products, sh), out_shape=[jax.Sha...]
where the time goes in v4:
time: 41.6 us; the launch traced here: 41.4 us
  Pallas kernels  37.1 us (89%)
  between operations  4.33 us (10%)
    pallas_call x1, Pallas kernels, sparse_path(): pl.pallas_call(functools.partial(sparse_products, sh), out_shape=[jax.Sha...  36.2 us
    pallas_call x1, Pallas kernels, deliver(): pl.pallas_call(kernel, out_shape=[half, half], in_specs=[VMEM], out_specs...  0.89 us

profile of v4, /device:TPU:0, one launch (start us, length us, event | category | flops | bytes accessed | tf_op | source)
XLA Modules:
  0.0 41.4 jit_solution(17833579434034089132)
XLA Ops:
  1.9 36.2 %sparse_products.1 = (bf16[24,128,128]{2,1,0:T(8,128)(2,1)S(1)}, f32[1,1]{1,0:T(1,128)}, f32[1,1]{1,0:T(1,128)}) custom-call(bf16[12,128,128]{2,1,0:T(8,128)(2,1)} %p_hbm.1, bf16[12,128,128]{2,1,0:T(8,128)(2,1)} %h_hbm.1, s32[2,12]{1,0:T(2,128)} %bitcast.22, s32[1,1]{1,0:T(1,128)S(6)} %copy.16.pc_hbm, s32[2,12]{1,0:T(2,128)} %bitcast.23, s32[1,1]{1,0:T(1,128)S(6)} %copy.17.hc_hbm), custom_call_target="tpu_custom_call" | custom-call | tf_op jit(solution)/shard_map/sparse_products/pallas_call | solution.py:1126
  38.7 0.9 %conditional.1 = (bf16[12,128,128]{2,1,0:T(8,128)(2,1)}, bf16[12,128,128]{2,1,0:T(8,128)(2,1)}, f32[1,1]{1,0:T(1,128)}) conditional(s32[]{:T(128)} %bitcast.12, (bf16[24,128,128]{2,1,0:T(8,128)(2,1)S(1)}, f32[1,1]{1,0:T(1,128)}) %tuple.15, (s32[12,2]{0,1:T(2,128)}, s32[12,2]{0,1:T(2,128)}, s32[1,1]{1,0:T(1,128)}, s32[1,1]{1,0:T(1,128)}, ...), branch_computations={%region_0.0_spmd, %region_1.2_spmd} | conditional | bytes 1579024 | solution.py:1209
  38.7 0.9 %deliver.1 = (bf16[12,128,128]{2,1,0:T(8,128)(2,1)}, bf16[12,128,128]{2,1,0:T(8,128)(2,1)}) custom-call(bf16[24,128,128]{2,1,0:T(8,128)(2,1)S(1)} %get-tuple-element.16.both_ref), custom_call_target="tpu_custom_call" | custom-call | tf_op jit(solution)/shard_map/cond/branch_0_fun/deliver/pallas_call | solution.py:1193

commit v5 on v4

--- a/solution.py
+++ b/solution.py
@@ -1092,7 +1092,7 @@
         out[slots + s] = entry(terms_2, tab, 3, 96 + s).astype(BF16)
 
     bulk(emsgs, e_recv).wait()
-    e_out[0, 0] = jnp.sum(jnp.sum(emsgs[:, 0], axis=0))
+    e_out[...] = jnp.sum(jnp.sum(emsgs[:, 0], axis=0), axis=1, keepdims=True) + jnp.zeros((8, 128), F32)
     over_out[0, 0] = jnp.sum(jnp.sum(emsgs[:, 1], axis=0))
 
     bulk(messages, m_send).wait()
@@ -1125,9 +1125,9 @@
     scalar = jax.ShapeDtypeStruct((1, 1), F32)
     return pl.pallas_call(
         functools.partial(sparse_products, sh),
-        out_shape=[jax.ShapeDtypeStruct((2 * slots,) + block, BF16), scalar, scalar],
+        out_shape=[jax.ShapeDtypeStruct((2 * slots,) + block, BF16), jax.ShapeDtypeStruct((8, 128), F32), scalar],
         in_specs=[ANY] * 6,
-        out_specs=[VMEM, SMEM, SMEM],
+        out_specs=[VMEM, VMEM, SMEM],
         scratch_shapes=[
             bf(slots, *block),
             bf(slots, *block),
@@ -1177,13 +1177,16 @@
     )(p_values, h_values, p_where.T, p_count, h_where.T, h_count)
 
 
-def deliver(both):
-    def kernel(both_ref, first, second, sems):
+def deliver(both, energy):
+    def kernel(both_ref, e_in, first, second, e_out, e_one, sems):
         slots = first.shape[0]
-        copies = [
-            pltpu.make_async_copy(both_ref.at[pl.ds(k * slots, slots)], ref, sems.at[k])
-            for k, ref in enumerate((first, second))
-        ]
+        e_one[...] = e_in[0:1, 0:1]
+        moves = (
+            (both_ref.at[pl.ds(0, slots)], first),
+            (both_ref.at[pl.ds(slots, slots)], second),
+            (e_one, e_out),
+        )
+        copies = [pltpu.make_async_copy(*move, sems.at[k]) for k, move in enumerate(moves)]
         for copy in copies:
             copy.start()
         for copy in copies:
@@ -1192,12 +1195,12 @@
     half = jax.ShapeDtypeStruct((both.shape[0] // 2,) + both.shape[1:], both.dtype)
     return pl.pallas_call(
         kernel,
-        out_shape=[half, half],
-        in_specs=[VMEM],
-        out_specs=[ANY, ANY],
-        scratch_shapes=[pltpu.SemaphoreType.DMA((2,))],
+        out_shape=[half, half, jax.ShapeDtypeStruct((1, 1), F32)],
+        in_specs=[VMEM, VMEM],
+        out_specs=[ANY, ANY, ANY],
+        scratch_shapes=[pltpu.VMEM((1, 1), F32), pltpu.SemaphoreType.DMA((3,))],
         name="deliver",
-    )(both)
+    )(both, energy)
 
 
 def per_device(rows, cols, *args):
@@ -1206,11 +1209,12 @@
     if not sh.fits():
         return dense_path(rows, cols, *args)
     both, energy, over = sparse_path(sh, *args)
-    return lax.cond(
-        over[0, 0] > 0.0,
-        lambda: dense_path(rows, cols, *args),
-        lambda: (*deliver(both), energy[0, 0]),
-    )
+    def dense():
+        ph, php, total = dense_path(rows, cols, *args)
+        return ph, php, total.reshape((1, 1))
+
+    ph, php, energy = lax.cond(over[0, 0] > 0.0, dense, lambda: tuple(deliver(both, energy)))
+    return ph, php, energy[0, 0]
 
 
 def solution(mesh):

time: 41.6 us -> 39.8 us (0.957)
  between operations: 4.33 us -> 2.57 us
where the time goes in v5:
time: 39.8 us; the launch traced here: 39.6 us
  Pallas kernels  37.1 us (93%)
  between operations  2.57 us (6%)
    pallas_call x1, Pallas kernels, sparse_path(): pl.pallas_call(functools.partial(sparse_products, sh), out_shape=[jax.Sha...  36.1 us
    pallas_call x1, Pallas kernels, deliver(): pl.pallas_call(kernel, out_shape=[half, half, jax.ShapeDtypeStruct((1, 1)...  0.91 us

profile of v5, /device:TPU:0, one launch (start us, length us, event | category | flops | bytes accessed | tf_op | source)
XLA Modules:
  0.0 39.6 jit_solution(18282971911100072465)
XLA Ops:
  1.9 36.1 %sparse_products.1 = (bf16[24,128,128]{2,1,0:T(8,128)(2,1)S(1)}, f32[8,128]{1,0:T(8,128)S(1)}, f32[1,1]{1,0:T(1,128)}) custom-call(bf16[12,128,128]{2,1,0:T(8,128)(2,1)} %p_hbm.1, bf16[12,128,128]{2,1,0:T(8,128)(2,1)} %h_hbm.1, s32[2,12]{1,0:T(2,128)} %bitcast.23, s32[1,1]{1,0:T(1,128)S(6)} %copy.15.pc_hbm, s32[2,12]{1,0:T(2,128)} %bitcast.24, ...), custom_call_target="tpu_custom_call" | custom-call | tf_op jit(solution)/shard_map/sparse_products/pallas_call | solution.py:1126
  38.7 0.9 %conditional.1 = (bf16[12,128,128]{2,1,0:T(8,128)(2,1)}, bf16[12,128,128]{2,1,0:T(8,128)(2,1)}, f32[]{:T(128)}) conditional(s32[]{:T(128)} %bitcast.14, (bf16[24,128,128]{2,1,0:T(8,128)(2,1)S(1)}, f32[8,128]{1,0:T(8,128)S(1)}) %tuple.17, (s32[12,2]{0,1:T(2,128)}, s32[12,2]{0,1:T(2,128)}, s32[1,1]{1,0:T(1,128)}, s32[1,1]{1,0:T(1,128)}, ...), branch_computations={%region_0.0_spmd, %region_1.2_spmd} | conditional | bytes 3151916 | solution.py:1216
  38.7 0.9 %deliver.1 = (bf16[12,128,128]{2,1,0:T(8,128)(2,1)}, bf16[12,128,128]{2,1,0:T(8,128)(2,1)}, f32[1,1]{1,0:T(1,128)}) custom-call(bf16[24,128,128]{2,1,0:T(8,128)(2,1)S(1)} %get-tuple-element.20.both_ref, f32[8,128]{1,0:T(8,128)S(1)} %get-tuple-element.21.e_in), custom_call_target="tpu_custom_call" | custom-call | tf_op jit(solution)/shard_map/cond/branch_0_fun/deliver/pallas_call | solution.py:1196

commit v6 on v5

--- a/solution.py
+++ b/solution.py
@@ -457,7 +457,7 @@
     return (ph_values, php_values, energy[0, 0])
 
 
-CAP_H_Z, CAP_P_Z = 17, 12
+CAP_H_Z, CAP_P_Z = 16, 12
 CAP_H, CAP_P = 14, 9
 CAP_R, CAP_V, CAP_D = 7, 7, 3
 CAP_1, CAP_2 = 18, 12

time: 39.8 us -> 39.8 us (level)
  no operation moved by 1% of the time
where the time goes in v6:
time: 39.8 us; the launch traced here: 39.7 us
  Pallas kernels  37.1 us (93%)
  between operations  2.57 us (6%)
    pallas_call x1, Pallas kernels, sparse_path(): pl.pallas_call(functools.partial(sparse_products, sh), out_shape=[jax.Sha...  36.2 us
    pallas_call x1, Pallas kernels, deliver(): pl.pallas_call(kernel, out_shape=[half, half, jax.ShapeDtypeStruct((1, 1)...  0.91 us

profile of v6, /device:TPU:0, one launch (start us, length us, event | category | flops | bytes accessed | tf_op | source)
XLA Modules:
  0.0 39.7 jit_solution(5383862811214346519)
XLA Ops:
  1.9 36.2 %sparse_products.1 = (bf16[24,128,128]{2,1,0:T(8,128)(2,1)S(1)}, f32[8,128]{1,0:T(8,128)S(1)}, f32[1,1]{1,0:T(1,128)}) custom-call(bf16[12,128,128]{2,1,0:T(8,128)(2,1)} %p_hbm.1, bf16[12,128,128]{2,1,0:T(8,128)(2,1)} %h_hbm.1, s32[2,12]{1,0:T(2,128)} %bitcast.23, s32[1,1]{1,0:T(1,128)S(6)} %copy.15.pc_hbm, s32[2,12]{1,0:T(2,128)} %bitcast.24, ...), custom_call_target="tpu_custom_call" | custom-call | tf_op jit(solution)/shard_map/sparse_products/pallas_call | solution.py:1126
  38.7 0.9 %conditional.1 = (bf16[12,128,128]{2,1,0:T(8,128)(2,1)}, bf16[12,128,128]{2,1,0:T(8,128)(2,1)}, f32[]{:T(128)}) conditional(s32[]{:T(128)} %bitcast.14, (bf16[24,128,128]{2,1,0:T(8,128)(2,1)S(1)}, f32[8,128]{1,0:T(8,128)S(1)}) %tuple.17, (s32[12,2]{0,1:T(2,128)}, s32[12,2]{0,1:T(2,128)}, s32[1,1]{1,0:T(1,128)}, s32[1,1]{1,0:T(1,128)}, ...), branch_computations={%region_0.0_spmd, %region_1.2_spmd} | conditional | bytes 3151916 | solution.py:1216
  38.7 0.9 %deliver.1 = (bf16[12,128,128]{2,1,0:T(8,128)(2,1)}, bf16[12,128,128]{2,1,0:T(8,128)(2,1)}, f32[1,1]{1,0:T(1,128)}) custom-call(bf16[24,128,128]{2,1,0:T(8,128)(2,1)S(1)} %get-tuple-element.20.both_ref, f32[8,128]{1,0:T(8,128)S(1)} %get-tuple-element.21.e_in), custom_call_target="tpu_custom_call" | custom-call | tf_op jit(solution)/shard_map/cond/branch_0_fun/deliver/pallas_call | solution.py:1196
